TPU v7x, 512 devices: a whole 4x4x16 slice. The times are simulated.
512 devices in a mesh: seq: 32 (over z, core), ch: 16 (over x, y).
Axes of the slice: x: 4, y: 4, z: 16, core: 2. Of those that a mesh axis runs over, the one named last changes fastest.
Arguments:
- input_q: bfloat16 [16384, 8192], P('seq', 'ch'), may hold values from -6 to 6
- input_k: bfloat16 [16384, 8192], P('seq', 'ch'), may hold values from -6 to 6
- input_v: bfloat16 [16384, 8192], P('seq', 'ch'), may hold values from -6 to 6
- grad_out: bfloat16 [16384, 8192], P('seq', 'ch'), may hold values from -6 to 6
- short_filters: float32 [3, 3, 8192], P(None, None, 'ch'), may hold values from -3.5 to 3.5
- long_filter: float32 [128, 8192], P(None, 'ch'), may hold values from -0.5 to 0.5
- skip_gain: float32 [8192], P('ch'), may hold values from 0.5 to 1.5
Outputs:
- grad_input_q: bfloat16 [16384, 8192], P('seq', 'ch')
- grad_input_k: bfloat16 [16384, 8192], P('seq', 'ch')
- grad_input_v: bfloat16 [16384, 8192], P('seq', 'ch')
- grad_long: float32 [128, 8192], P('seq', 'ch')
- grad_short: float32 [3, 3, 8192], P(None, None, 'ch')
- grad_skip: float32 [8192], P('ch')
All inputs are finite; a program needn't handle non-finite values.
Results may differ from a plain program's by a relative error of at most 0.001.
Values may be sent and summed in bfloat16 or wider, within the bound.
A program may use at most 64 MiB of HBM per device.

v0:
```python
import jax
import jax.numpy as jnp
from jax import lax
from jax.sharding import PartitionSpec as P


def shifted(value, axis, by):
    size = lax.axis_size(axis)
    pairs = [(i, i + by) for i in range(size) if 0 <= i + by < size]
    return lax.ppermute(value, axis, pairs)


def in_blocks(value, dim, size):
    shape = value.shape
    pieces = value.reshape(*shape[:dim], size, shape[dim] // size, *shape[dim + 1 :])
    return jnp.moveaxis(pieces, dim, 0)


def sum_at_owner(value, axis, dim):
    pieces = in_blocks(value, dim, lax.axis_size(axis))
    arrived = lax.all_to_all(pieces, axis, split_axis=0, concat_axis=0, tiled=True)
    return arrived.sum(axis=0)


def sent_to_all(value, axis):
    size = lax.axis_size(axis)
    return lax.all_to_all(
        jnp.broadcast_to(value[None], (size, *value.shape)), axis, 0, 0, tiled=True
    )


def taken_together(value, axis):
    everything = sent_to_all(value, axis)
    return jnp.sum(everything, axis=0)


def depth_conv(signal, kernel):
    result = lax.conv_general_dilated(
        signal[None],
        kernel[:, None, :],
        (1,),
        "VALID",
        dimension_numbers=("NWC", "WIO", "NWC"),
        feature_group_count=signal.shape[1],
        precision=lax.Precision.HIGHEST,
    )
    return result[0]


def causal_filter(extended, filt):
    return depth_conv(extended, filt[::-1])


def later_filter(extended, filt):
    return depth_conv(extended, filt)


def tap_gradient(extended, grad):
    return depth_conv(extended, grad)[::-1]


def body(input_q, input_k, input_v, grad_out, short_filters, long_filter, skip_gain):
    length = input_q.shape[0]
    ntap = short_filters.shape[1]
    span = long_filter.shape[0]
    reach = span + ntap - 2
    own_q = input_q.astype(jnp.float32)
    own_k = input_k.astype(jnp.float32)
    own_v = input_v.astype(jnp.float32)
    k_tail = causal_filter(own_k[length - reach :], short_filters[1])
    v_tail = causal_filter(own_v[length - reach :], short_filters[2])
    stacked = jnp.stack(
        [own_q[length - (ntap - 1) :], own_k[length - (ntap - 1) :], own_v[length - (ntap - 1) :]]
    )
    before_z, before_u = shifted((k_tail * v_tail, stacked), "seq", 1)
    ext_q = jnp.concatenate([before_u[0], own_q], 0)
    ext_k = jnp.concatenate([before_u[1], own_k], 0)
    ext_v = jnp.concatenate([before_u[2], own_v], 0)
    q_feat = causal_filter(ext_q, short_filters[0])
    k_feat = causal_filter(ext_k, short_filters[1])
    v_feat = causal_filter(ext_v, short_filters[2])
    z_ext = jnp.concatenate([before_z, k_feat * v_feat], 0)
    z_feat = z_ext[span - 1 :]
    s_feat = causal_filter(z_ext, long_filter) + skip_gain * z_feat
    upstream = grad_out.astype(jnp.float32)
    grad_q = upstream * s_feat
    grad_s = upstream * q_feat
    after_s, after_q = shifted((grad_s[: span - 1], grad_q[: ntap - 1]), "seq", -1)
    grad_z = later_filter(jnp.concatenate([grad_s, after_s], 0), long_filter) + skip_gain * grad_s
    grad_k = grad_z * v_feat
    grad_v = grad_z * k_feat
    after_kv = shifted(jnp.stack([grad_k[: ntap - 1], grad_v[: ntap - 1]]), "seq", -1)
    grad_k_ext = jnp.concatenate([grad_k, after_kv[0]], 0)
    grad_v_ext = jnp.concatenate([grad_v, after_kv[1]], 0)
    grad_q_ext = jnp.concatenate([grad_q, after_q], 0)
    back_q = later_filter(grad_q_ext, short_filters[0]).astype(jnp.bfloat16)
    back_k = later_filter(grad_k_ext, short_filters[1]).astype(jnp.bfloat16)
    back_v = later_filter(grad_v_ext, short_filters[2]).astype(jnp.bfloat16)
    part_filt = tap_gradient(z_ext, grad_s)
    part_taps = jnp.stack(
        [
            tap_gradient(ext_q, grad_q),
            tap_gradient(ext_k, grad_k_ext[:length]),
            tap_gradient(ext_v, grad_v_ext[:length]),
        ]
    )
    part_gain = jnp.sum(grad_s * z_feat, axis=0)
    grad_filt = sum_at_owner(part_filt, "seq", 0)
    grad_taps, grad_gain = (taken_together(part_taps, "seq"), taken_together(part_gain, "seq"))
    return (back_q, back_k, back_v, grad_filt, grad_taps, grad_gain)


def solution(mesh):
    return jax.shard_map(
        body,
        mesh=mesh,
        in_specs=(
            P("seq", "ch"),
            P("seq", "ch"),
            P("seq", "ch"),
            P("seq", "ch"),
            P(None, None, "ch"),
            P(None, "ch"),
            P("ch"),
        ),
        out_specs=(
            P("seq", "ch"),
            P("seq", "ch"),
            P("seq", "ch"),
            P("seq", "ch"),
            P(None, None, "ch"),
            P("ch"),
        ),
        check_vma=False,
    )
```

profile of v0, /device:TPU:1, one launch (start us, length us, event | category | flops | bytes accessed | tf_op | source)
XLA Modules:
  0.0 176.8 jit_solution(15030070395586512228)
XLA Ops:
  0.6 1.2 convert_element_type.31
  4.0 4.9 %collective-permute-start.1 = (f32[3,2,512]{2,1,0:T(2,128)S(1)}, f32[3,2,512]{2,1,0:T(2,128)S(1)}, u32[]{:S(2)}, u32[]{:S(2)}) collective-permute-start(f32[3,2,512]{2,1,0:T(2,128)S(1)} %pad_maximum_fusion.3), channel_id=1, source_target_pairs={{0,16},{16,32},{32,48},{48,64},{64,80},{80,96},{96,112},{112,128},... | collective-permute-start | bytes 36872 | tf_op jit(solution)/shard_map/ppermute | solution.py:10
  10.9 1.9 %collective-permute-start = (f32[127,512]{1,0:T(8,128)}, f32[127,512]{1,0:T(8,128)}, u32[]{:S(2)}, u32[]{:S(2)}) collective-permute-start(f32[127,512]{1,0:T(8,128)} %slice_bitcast_fusion.6), channel_id=1, source_target_pairs={{0,16},{16,32},{32,48},{48,64},{64,80},{80,96},{96,112},{112,128},... | collective-permute-start | bytes 780296 | tf_op jit(solution)/shard_map/ppermute | solution.py:10
  13.0 1.3 rev.28
  14.5 1.5 copy-done.6
  19.3 1.2 reshape.67
  20.6 1.3 reshape.49
  23.1 1.3 reshape.42
  25.4 1.2 reshape.46
  26.6 2.1 %multiply_reduce_fusion = (f32[512]{0:T(512)S(1)}, f32[512,512]{1,0:T(8,128)S(1)}, f32[512,512]{1,0:T(8,128)S(1)}) fusion(f32[1,520,512]{2,1,0:T(8,128)} %reshape.67, bf16[512,512]{1,0:T(8,128)(2,1)} %param.10, f32[1,520,512]{2,1,0:T(8,128)S(1)} %reshape.53, f32[1,520,512]{2,1,0:T(8,128)} %reshape.46), kind=kLoop, calls=%fused_computation.64 | loop fusion | flops 1310208 | bytes 5769216 | tf_op jit(solution)/shard_map/reduce_sum | solution.py:107
  29.3 14.8 %all-to-all-start.2 = ((f32[32,1,512]{2,1,0:T(1,128)}), f32[32,1,512]{2,1,0:T(1,128)S(1)}, u32[]{:S(2)}, u32[]{:S(2)}) async-start(f32[32,1,512]{2,1,0:T(1,128)} %broadcast_in_dim.97), calls=%async_computation.2 | async-start | bytes 131072 | tf_op jit(solution)/shard_map/all_to_all | solution.py:27
  44.9 2.3 %collective-permute-start.3 = (f32[127,512]{1,0:T(8,128)}, f32[127,512]{1,0:T(8,128)}, u32[]{:S(2)}, u32[]{:S(2)}) collective-permute-start(f32[127,512]{1,0:T(8,128)} %slice.106), channel_id=1, source_target_pairs={{16,0},{32,16},{48,32},{64,48},{80,64},{96,80},{112,96},{128,112},... | collective-permute-start | bytes 780296 | tf_op jit(solution)/shard_map/ppermute | solution.py:10
  49.2 10.2 %fusion.38 = f32[1,128,512]{2,0,1:T(1,128)S(1)} fusion(f32[1,639,512]{2,0,1:T(1,128)S(1)} %broadcast_in_dim.83, f32[512,1,512]{2,0,1:T(8,128)S(1)} %bitcast.143), kind=kOutput, calls=%fused_computation.62 | convolution fusion | flops 402653184 | bytes 2619392 | tf_op jit(solution)/shard_map/conv_general_dilated | solution.py:38
  59.4 11.3 %fusion.58 = f32[1,512,512]{2,0,1:T(1,128)} fusion(f32[1,639,512]{2,0,1:T(1,128)S(1)} %broadcast_in_dim.83, f32[128,1,512]{2,0,1:T(8,128)S(1)} %bitcast.150), kind=kOutput, calls=%fused_computation.89 | convolution fusion | flops 402653184 | bytes 2619392 | tf_op jit(solution)/shard_map/conv_general_dilated | solution.py:38
  70.7 1.3 rev.30
  72.0 1.7 reshape.27
  73.8 12.2 %all-to-all-start = ((f32[32,4,512]{2,1,0:T(4,128)}), f32[32,4,512]{2,1,0:T(4,128)S(1)}, u32[]{:S(2)}, u32[]{:S(2)}) async-start(f32[32,4,512]{2,1,0:T(4,128)} %reshape.27), calls=%async_computation | async-start | bytes 524288 | tf_op jit(solution)/shard_map/all_to_all | solution.py:21
  87.8 11.2 %fusion = f32[1,512,512]{2,0,1:T(1,128)S(1)} fusion(f32[1,639,512]{2,1,0:T(8,128)S(1)} %maximum_bitcast_fusion, f32[128,1,512]{2,0,1:T(8,128)S(1)} %bitcast.149), kind=kOutput, calls=%fused_computation.10 | convolution fusion | flops 402653184 | bytes 2619392 | tf_op jit(solution)/shard_map/conv_general_dilated | solution.py:38
  99.1 2.1 %fusion.42 = (f32[512,512]{1,0:T(8,128)}, f32[512,512]{1,0:T(8,128)}, f32[512,512]{1,0:T(8,128)S(1)}) fusion(f32[1,520,512]{2,1,0:T(8,128)S(1)} %reshape.53, f32[512,512]{1,0:T(8,128)S(1)} %get-tuple-element.7, f32[512]{0:T(512)S(1)} %copy-done.22, f32[1,512,512]{2,0,1:T(1,128)S(1)} %fusion, f32[1,520,512]{2,1,0:T(8,128)S(1)} %copy-done, ...), kind=kLoop, calls=%fused_computation.67 | loop fusion | flops 2097152 | bytes 9963520 | tf_op jit(solution)/shard_map/mul | solution.py:90
  101.2 2.5 %fusion.36 = f32[1,3,512]{2,0,1:T(1,128)S(1)} fusion(f32[1,514,512]{2,0,1:T(1,128)S(1)} %copy-done.12, f32[512,1,512]{2,0,1:T(8,128)S(1)} %bitcast.147), kind=kOutput, calls=%fused_computation.60 | convolution fusion | flops 9437184 | bytes 2107392 | tf_op jit(solution)/shard_map/conv_general_dilated | solution.py:38
  103.9 5.2 %fusion.30 = f32[1,3,512]{2,0,1:T(1,128)S(1)} fusion(f32[1,514,512]{2,1,0:T(8,128)S(1)} %copy-done.4, f32[512,1,512]{2,0,1:T(8,128)} %bitcast.146), kind=kOutput, calls=%fused_computation.49 | convolution fusion | flops 9437184 | bytes 2107392 | tf_op jit(solution)/shard_map/conv_general_dilated | solution.py:38
  109.2 3.1 %fusion.32 = f32[1,3,512]{2,0,1:T(1,128)S(1)} fusion(f32[1,514,512]{2,1,0:T(8,128)S(1)} %copy-done.2, f32[512,1,512]{2,0,1:T(8,128)S(1)} %bitcast.145), kind=kOutput, calls=%fused_computation.51 | convolution fusion | flops 9437184 | bytes 2107392 | tf_op jit(solution)/shard_map/conv_general_dilated | solution.py:38
  113.5 12.2 %all-to-all-start.1 = ((f32[32,3,3,512]{3,2,1,0:T(4,128)}), f32[32,3,3,512]{3,2,1,0:T(4,128)}, u32[]{:S(2)}, u32[]{:S(2)}) async-start(f32[32,3,3,512]{3,2,1,0:T(4,128)} %broadcast_in_dim.96), calls=%async_computation.1 | async-start | bytes 1572864 | tf_op jit(solution)/shard_map/all_to_all | solution.py:27
  126.5 2.2 %collective-permute-start.2 = (f32[2,512]{1,0:T(2,128)S(1)}, f32[2,512]{1,0:T(2,128)S(1)}, u32[]{:S(2)}, u32[]{:S(2)}) collective-permute-start(f32[2,512]{1,0:T(2,128)S(1)} %slice.100), channel_id=1, source_target_pairs={{16,0},{32,16},{48,32},{64,48},{80,64},{96,80},{112,96},{128,112},... | collective-permute-start | bytes 12296 | tf_op jit(solution)/shard_map/ppermute | solution.py:10
  128.7 2.1 %collective-permute-start.4 = (f32[2,2,512]{2,1,0:T(2,128)S(1)}, f32[2,2,512]{2,1,0:T(2,128)S(1)}, u32[]{:S(2)}, u32[]{:S(2)}) collective-permute-start(f32[2,2,512]{2,1,0:T(2,128)S(1)} %pad_maximum_fusion.4), channel_id=1, source_target_pairs={{16,0},{32,16},{48,32},{64,48},{80,64},{96,80},{112,96},{128,112},... | collective-permute-start | bytes 24584 | tf_op jit(solution)/shard_map/ppermute | solution.py:10
  130.9 29.8 %collective-permute-done.2 = f32[2,512]{1,0:T(2,128)S(1)} collective-permute-done((f32[2,512]{1,0:T(2,128)S(1)}, f32[2,512]{1,0:T(2,128)S(1)}, u32[]{:S(2)}, u32[]{:S(2)}) %collective-permute-start.2) | collective-permute-done | bytes 4128 | tf_op jit(solution)/shard_map/ppermute | solution.py:10
  160.9 1.3 reshape.56
  164.3 1.9 %slice_bitcast_fusion.5 = bf16[512,512]{1,0:T(8,128)(2,1)} fusion(bf16[1,520,512]{2,1,0:T(8,128)(2,1)} %reshape.60), kind=kLoop, calls=%fused_computation.82 | loop fusion | bytes 1048576 | tf_op jit(solution)/shard_map/convert_element_type | solution.py:96
  166.3 1.3 reshape.77
  167.6 1.1 copy.148
  168.9 1.3 reshape.70
  174.9 1.9 %reduce_sum.37 = f32[3,3,512]{2,1,0:T(4,128)} reduce(f32[32,3,3,512]{3,2,1,0:T(4,128)} %all-to-all-done.1, f32[]{:T(128)} %constant.29.clone.1), dimensions={0}, to_apply=%region_1.0 | reduce | flops 142848 | bytes 608260 | tf_op jit(solution)/shard_map/reduce_sum | solution.py:34
  (146 shorter events, 24.4 us)
Async XLA Ops:
  0.6 1.3 copy-start.16
  1.9 1.0 copy-start.17
  2.9 6.1 %copy-start.21 = (f32[3,3,512]{2,1,0:T(4,128)S(1)}, f32[3,3,512]{2,1,0:T(4,128)}, u32[]{:S(2)}) copy-start(f32[3,3,512]{2,1,0:T(4,128)} %param.11) | copy-start | bytes 55300
  3.0 1.0 copy-start.5
  4.0 10.3 %collective-permute-start.1 = (f32[3,2,512]{2,1,0:T(2,128)S(1)}, f32[3,2,512]{2,1,0:T(2,128)S(1)}, u32[]{:S(2)}, u32[]{:S(2)}) collective-permute-start(f32[3,2,512]{2,1,0:T(2,128)S(1)} %pad_maximum_fusion.3), channel_id=1, source_target_pairs={{0,16},{16,32},{32,48},{48,64},{64,80},{80,96},{96,112},{112,128},... | collective-permute-start | bytes 36872 | tf_op jit(solution)/shard_map/ppermute | solution.py:10
  10.0 3.0 %copy-start.18 = (f32[128,512]{1,0:T(8,128)S(1)}, f32[128,512]{1,0:T(8,128)}, u32[]{:S(2)}) copy-start(f32[128,512]{1,0:T(8,128)} %param.12) | copy-start | bytes 786436
  10.9 36.3 %collective-permute-start = (f32[127,512]{1,0:T(8,128)}, f32[127,512]{1,0:T(8,128)}, u32[]{:S(2)}, u32[]{:S(2)}) collective-permute-start(f32[127,512]{1,0:T(8,128)} %slice_bitcast_fusion.6), channel_id=1, source_target_pairs={{0,16},{16,32},{32,48},{48,64},{64,80},{80,96},{96,112},{112,128},... | collective-permute-start | bytes 780296 | tf_op jit(solution)/shard_map/ppermute | solution.py:10
  14.3 1.6 copy-start.6
  14.5 8.6 %copy-start.1 = (f32[1,514,512]{2,1,0:T(8,128)}, f32[1,514,512]{2,1,0:T(8,128)S(1)}, u32[]{:S(2)}) copy-start(f32[1,514,512]{2,1,0:T(8,128)S(1)} %maximum_bitcast_fusion.1) | copy-start | bytes 3158020
  16.1 4.4 %copy-start.3 = (f32[1,514,512]{2,1,0:T(8,128)}, f32[1,514,512]{2,1,0:T(8,128)S(1)}, u32[]{:S(2)}) copy-start(f32[1,514,512]{2,1,0:T(8,128)S(1)} %maximum_bitcast_fusion.2) | copy-start | bytes 3158020
  16.9 1.0 copy-start.11
  17.7 0.7 copy-start.23
  29.3 44.5 %all-to-all-start.2 = ((f32[32,1,512]{2,1,0:T(1,128)}), f32[32,1,512]{2,1,0:T(1,128)S(1)}, u32[]{:S(2)}, u32[]{:S(2)}) async-start(f32[32,1,512]{2,1,0:T(1,128)} %broadcast_in_dim.97), calls=%async_computation.2 | async-start | bytes 131072 | tf_op jit(solution)/shard_map/all_to_all | solution.py:27
  44.9 41.8 %collective-permute-start.3 = (f32[127,512]{1,0:T(8,128)}, f32[127,512]{1,0:T(8,128)}, u32[]{:S(2)}, u32[]{:S(2)}) collective-permute-start(f32[127,512]{1,0:T(8,128)} %slice.106), channel_id=1, source_target_pairs={{16,0},{32,16},{48,32},{64,48},{80,64},{96,80},{112,96},{128,112},... | collective-permute-start | bytes 780296 | tf_op jit(solution)/shard_map/ppermute | solution.py:10
  49.2 10.2 %copy-start.20 = (f32[128,512]{1,0:T(8,128)S(1)}, f32[128,512]{1,0:T(8,128)}, u32[]{:S(2)}) copy-start(f32[128,512]{1,0:T(8,128)} %rev.28) | copy-start | bytes 786436
  73.8 38.7 %all-to-all-start = ((f32[32,4,512]{2,1,0:T(4,128)}), f32[32,4,512]{2,1,0:T(4,128)S(1)}, u32[]{:S(2)}, u32[]{:S(2)}) async-start(f32[32,4,512]{2,1,0:T(4,128)} %reshape.27), calls=%async_computation | async-start | bytes 524288 | tf_op jit(solution)/shard_map/all_to_all | solution.py:21
  86.6 1.1 copy-start.19
  87.7 11.3 %copy-start = (f32[1,520,512]{2,1,0:T(8,128)S(1)}, f32[1,520,512]{2,1,0:T(8,128)}, u32[]{:S(2)}) copy-start(f32[1,520,512]{2,1,0:T(8,128)} %reshape.46) | copy-start | bytes 3194884
  87.7 11.3 %copy-start.13 = (bf16[512,512]{1,0:T(8,128)(2,1)S(1)}, bf16[512,512]{1,0:T(8,128)(2,1)}, u32[]{:S(2)}) copy-start(bf16[512,512]{1,0:T(8,128)(2,1)} %param.10) | copy-start | bytes 1572868
  87.8 11.3 %copy-start.15 = (f32[1,512,512]{2,0,1:T(1,128)S(1)}, f32[1,512,512]{2,0,1:T(1,128)}, u32[]{:S(2)}) copy-start(f32[1,512,512]{2,0,1:T(1,128)} %fusion.58) | copy-start | bytes 3145732
  87.8 11.3 %copy-start.22 = (f32[512]{0:T(512)S(1)}, f32[512]{0:T(512)}, u32[]{:S(2)}) copy-start(f32[512]{0:T(512)} %param.13) | copy-start | bytes 6148
  99.1 2.1 %copy-start.12 = (f32[1,514,512]{2,0,1:T(1,128)S(1)}, f32[1,514,512]{2,0,1:T(1,128)}, u32[]{:S(2)}) copy-start(f32[1,514,512]{2,0,1:T(1,128)} %copy-done.11) | copy-start | bytes 3158020
  101.2 2.5 %copy-start.9 = (f32[512,512]{1,0:T(8,128)}, f32[512,512]{1,0:T(8,128)S(1)}, u32[]{:S(2)}) copy-start(f32[512,512]{1,0:T(8,128)S(1)} %get-tuple-element.22) | copy-start | bytes 3145732
  101.2 2.6 %copy-start.4 = (f32[1,514,512]{2,1,0:T(8,128)S(1)}, f32[1,514,512]{2,1,0:T(8,128)}, u32[]{:S(2)}) copy-start(f32[1,514,512]{2,1,0:T(8,128)} %copy-done.3) | copy-start | bytes 3158020
  103.9 5.4 %copy-start.2 = (f32[1,514,512]{2,1,0:T(8,128)S(1)}, f32[1,514,512]{2,1,0:T(8,128)}, u32[]{:S(2)}) copy-start(f32[1,514,512]{2,1,0:T(8,128)} %copy-done.1) | copy-start | bytes 3158020
  103.9 5.4 %copy-start.7 = (f32[512,512]{1,0:T(8,128)S(1)}, f32[512,512]{1,0:T(8,128)}, u32[]{:S(2)}) copy-start(f32[512,512]{1,0:T(8,128)} %get-tuple-element.9) | copy-start | bytes 3145732
  112.5 14.0 %copy-start.10 = (f32[512,512]{1,0:T(8,128)S(1)}, f32[512,512]{1,0:T(8,128)}, u32[]{:S(2)}) copy-start(f32[512,512]{1,0:T(8,128)} %copy-done.9) | copy-start | bytes 3145732
  113.5 61.4 %all-to-all-start.1 = ((f32[32,3,3,512]{3,2,1,0:T(4,128)}), f32[32,3,3,512]{3,2,1,0:T(4,128)}, u32[]{:S(2)}, u32[]{:S(2)}) async-start(f32[32,3,3,512]{3,2,1,0:T(4,128)} %broadcast_in_dim.96), calls=%async_computation.1 | async-start | bytes 1572864 | tf_op jit(solution)/shard_map/all_to_all | solution.py:27
  126.5 34.2 %collective-permute-start.2 = (f32[2,512]{1,0:T(2,128)S(1)}, f32[2,512]{1,0:T(2,128)S(1)}, u32[]{:S(2)}, u32[]{:S(2)}) collective-permute-start(f32[2,512]{1,0:T(2,128)S(1)} %slice.100), channel_id=1, source_target_pairs={{16,0},{32,16},{48,32},{64,48},{80,64},{96,80},{112,96},{128,112},... | collective-permute-start | bytes 12296 | tf_op jit(solution)/shard_map/ppermute | solution.py:10
  128.7 37.4 %collective-permute-start.4 = (f32[2,2,512]{2,1,0:T(2,128)S(1)}, f32[2,2,512]{2,1,0:T(2,128)S(1)}, u32[]{:S(2)}, u32[]{:S(2)}) collective-permute-start(f32[2,2,512]{2,1,0:T(2,128)S(1)} %pad_maximum_fusion.4), channel_id=1, source_target_pairs={{16,0},{32,16},{48,32},{64,48},{80,64},{96,80},{112,96},{128,112},... | collective-permute-start | bytes 24584 | tf_op jit(solution)/shard_map/ppermute | solution.py:10
  163.3 2.9 %copy-start.8 = (f32[512,512]{1,0:T(8,128)S(1)}, f32[512,512]{1,0:T(8,128)}, u32[]{:S(2)}) copy-start(f32[512,512]{1,0:T(8,128)} %get-tuple-element.10) | copy-start | bytes 3145732
  170.1 1.2 copy-start.14
  (2 other events, 1.4 us)
where the time goes:
time: 178 us; the launch traced here: 177 us
  starting transfers between devices  52.8 us (30%)
  matrix products  45.2 us (25%)
  local copies, waits for them, and re-layouts  35.8 us (20%)
  waiting for transfers between devices  29.8 us (17%)
  other arithmetic  11.6 us (7%)
    conv_general_dilated x14, matrix products, depth_conv(): lax.conv_general_dilated(signal[None], kernel[:, None, :], (1,), 'VALID',...  45.2 us
    ppermute x5, waiting for transfers between devices, shifted(): return lax.ppermute(value, axis, pairs)  29.8 us
    all_to_all x2, starting transfers between devices, sent_to_all(): lax.all_to_all(jnp.broadcast_to(value[None], (size, *value.shape)), axis,...  27.1 us
    ppermute x5, starting transfers between devices, shifted(): return lax.ppermute(value, axis, pairs)  13.5 us
    conv_general_dilated x29, local copies, waits for them, and re-layouts, depth_conv(): lax.conv_general_dilated(signal[None], kernel[:, None, :], (1,), 'VALID',...  12.6 us
    all_to_all x1, starting transfers between devices, sum_at_owner(): lax.all_to_all(pieces, axis, split_axis=0, concat_axis=0, tiled=True)  12.2 us
    unnamed x56, local copies, waits for them, and re-layouts  5.77 us
  transfers between devices with their start and end apart: 8, of which 1 were waited for; matrix products, arithmetic and copies ran while one was open for 47% of the time, Pallas kernels for 0%

commit v1 on v0

v1 whole, which is shorter than its diff:
```python
import functools

import jax
import jax.numpy as jnp
import ml_dtypes
import numpy as np
from jax import lax
from jax.experimental import pallas as pl
from jax.experimental.pallas import tpu as pltpu
from jax.sharding import PartitionSpec as P

F32, BF16 = jnp.float32, jnp.bfloat16
BLK = 128
ROWS = 16


def tables():
    order = np.concatenate([np.arange(0, BLK, 2), np.arange(1, BLK, 2)])
    angle = np.outer(np.pi * (2 * order + 1) / (2 * BLK), np.arange(BLK))
    full = np.concatenate([np.cos(angle), -np.sin(angle)], 0)
    high = full.astype(ml_dtypes.bfloat16).astype(np.float64)
    low = full - high
    fwd = np.concatenate([high, high, low], 1)
    inv = np.concatenate([high.T, high.T, low.T], 1) / BLK
    return fwd.astype(ml_dtypes.bfloat16), inv.astype(ml_dtypes.bfloat16)


def kernel(
    chips,
    q_hbm, k_hbm, v_hbm, y_hbm, sf_hbm, lf_hbm, sg_hbm, fwd_hbm, inv_hbm,
    oq, ok, ov, ofilt, otaps, ogain,
    qb, kb, vb, yb, nq, ny, sf, lf, sg, fwd, inv,
    kf, vf, s_t, gz_t, xz, xg, xh, zs, gs, hs, xs, xu, gl_f, xgl,
    mine3, nx, glt, gl_in, racc, rs_in, small, half, half_in, ar, fin,
    in_sem, send, recv, known,
):
    length = q_hbm.shape[0]
    width = q_hbm.shape[1]
    nblk = length // BLK
    me = lax.axis_index("seq")
    total = 2 * chips
    z, c = me // 2, lax.rem(me, 2)
    has_prev, has_next = me > 0, me < total - 1
    prev, nxt = me - 1, me + 1
    partner = me + 1 - 2 * c

    def at_chip(chip):
        return lax.rem(chip + chips, chips) * 2 + c

    def remote(src, dst, slot, device):
        return pltpu.make_async_remote_copy(
            src_ref=src, dst_ref=dst, send_sem=send.at[slot], recv_sem=recv.at[slot],
            device_id={"seq": device}, device_id_type=pl.DeviceIdType.MESH,
        )

    def signal(sem, device):
        pl.semaphore_signal(sem, 1, device_id={"seq": device}, device_id_type=pl.DeviceIdType.MESH)

    def load(array, b):
        hbm, buf = ((q_hbm, qb), (k_hbm, kb), (v_hbm, vb), (y_hbm, yb))[array]
        off = 0 if array == 3 else ROWS
        return pltpu.make_async_copy(
            hbm.at[pl.ds(b * BLK, BLK)], buf.at[pl.ds(off + b * BLK, BLK)], in_sem.at[array * nblk + b]
        )

    extra = []
    for n, (hbm, buf) in enumerate(((sf_hbm, sf), (lf_hbm, lf), (sg_hbm, sg), (fwd_hbm, fwd), (inv_hbm, inv))):
        extra.append(pltpu.make_async_copy(hbm, buf, in_sem.at[4 * nblk + n]))

    last = nblk - 1
    barrier = pltpu.get_barrier_semaphore()
    extra[0].start()
    for b in (last - 1, last):
        load(1, b).start()
        load(2, b).start()
    signal(barrier, at_chip(z + 1))
    signal(barrier, at_chip(z - 1))

    @pl.when(has_prev)
    def _():
        signal(barrier, prev)

    @pl.when(has_next)
    def _():
        signal(barrier, nxt)

    load(0, 0).start()
    load(3, 0).start()
    extra[1].start()
    extra[2].start()
    extra[3].start()
    load(0, last).start()
    for b in range(nblk):
        for array in range(4):
            if not (array in (1, 2) and b >= last - 1) and not (array in (0, 3) and b == 0) and not (array == 0 and b == last):
                load(array, b).start()
    extra[4].start()

    @pl.when(jnp.logical_not(has_prev))
    def _():
        for buf in (qb, kb, vb):
            buf[0:ROWS, :] = jnp.zeros((ROWS, width), BF16)
        xz[0, 0 : 2 * BLK, :] = jnp.zeros((2 * BLK, width), BF16)

    @pl.when(jnp.logical_not(has_next))
    def _():
        nq[...] = jnp.zeros_like(nq)
        ny[...] = jnp.zeros_like(ny)
        xg[nblk, 0 : 2 * BLK, :] = jnp.zeros((2 * BLK, width), BF16)
        nx[...] = jnp.zeros_like(nx)

    def delayed(now, before):
        cat = jnp.concatenate([before.astype(F32)[8:], now.astype(F32)], 0)
        return cat[8:], pltpu.roll(cat, 1, 0)[8:], pltpu.roll(cat, 2, 0)[8:]

    def feat(now, before, which):
        own, one, two = delayed(now, before)
        return sf[which, 0:1, :] * own + sf[which, 1:2, :] * one + sf[which, 2:3, :] * two

    def put(ref, b, n, value):
        high = value.astype(BF16)
        low = (value - high.astype(F32)).astype(BF16)
        ref[b, pl.ds(n, ROWS), :] = high
        ref[b, pl.ds(BLK + n, ROWS), :] = low
        ref[b, pl.ds(2 * BLK + n, ROWS), :] = high

    def z_chunk(b, n):
        row = b * BLK + n
        kk = feat(kb[pl.ds(row + ROWS, ROWS), :], kb[pl.ds(row, ROWS), :], 1)
        vv = feat(vb[pl.ds(row + ROWS, ROWS), :], vb[pl.ds(row, ROWS), :], 2)
        kf[pl.ds(row, ROWS), :] = kk
        vf[pl.ds(row, ROWS), :] = vv
        put(xz, b + 1, n, kk * vv)

    def g_chunk(b, n):
        row = b * BLK + n
        qq = feat(qb[pl.ds(row + ROWS, ROWS), :], qb[pl.ds(row, ROWS), :], 0)
        put(xg, b, n, yb[pl.ds(row, ROWS), :].astype(F32) * qq)

    def chunks(body, first, stop):
        def step(i, carry):
            body(pl.multiple_of(i * ROWS, ROWS))
            return carry

        lax.fori_loop(first, stop, step, 0)

    per = BLK // ROWS
    extra[0].wait()
    for b in (last - 1, last):
        load(1, b).wait()
        load(2, b).wait()
    chunks(lambda n: z_chunk(last, n), 0, per)
    load(0, 0).wait()
    load(3, 0).wait()
    chunks(lambda n: g_chunk(0, n), 1, per)
    load(0, last).wait()

    count = 2 + has_prev.astype(jnp.int32) + has_next.astype(jnp.int32)
    pl.semaphore_wait(barrier, count)
    tail = pl.ds(length, ROWS)
    to_next = [remote(buf.at[tail], buf.at[pl.ds(0, ROWS)], n, nxt) for n, buf in enumerate((qb, kb, vb))]
    z_halo = remote(xz.at[nblk, pl.ds(0, 2 * BLK)], xz.at[0, pl.ds(0, 2 * BLK)], 3, nxt)
    to_prev = [
        remote(qb.at[pl.ds(ROWS, ROWS)], nq, 4, prev),
        remote(yb.at[pl.ds(0, ROWS)], ny, 5, prev),
    ]
    g_halo = [
        remote(xg.at[0, pl.ds(h * BLK + ROWS, BLK - ROWS)], xg.at[nblk, pl.ds(h * BLK + ROWS, BLK - ROWS)], 6 + h, prev)
        for h in range(2)
    ]

    @pl.when(has_next)
    def _():
        for copy in to_next:
            copy.start()
        z_halo.start()

    @pl.when(has_prev)
    def _():
        for copy in to_prev + g_halo:
            copy.start()

    steps = []
    radius = 1
    while radius < chips // 2:
        steps.append(radius)
        radius *= 2

    def tell(n):
        if n < len(steps):
            signal(known.at[n], at_chip(z + steps[n]))
            signal(known.at[n], at_chip(z - steps[n]))

    def learn(n):
        if n < len(steps):
            pl.semaphore_wait(known.at[n], 2)

    tell(0)

    extra[1].wait()
    extra[2].wait()

    def h_chunk(n):
        put(xh, 0, n, lf[pl.ds(n, ROWS), :])

    chunks(h_chunk, 1, per)
    first = lf[0:ROWS, :]
    at_zero = lax.broadcasted_iota(jnp.int32, (ROWS, width), 0) == 0
    put(xh, 0, 0, jnp.where(at_zero, first + sg[...], first))
    extra[3].wait()

    def dft(x, b, out, o):
        for lane in range(0, width, 256):
            cols = slice(lane, lane + 256)
            out[o, :, cols] = jnp.dot(fwd[...], x[b, :, cols], preferred_element_type=F32)

    def inverse(x, b):
        return jnp.dot(inv[...], x[b], preferred_element_type=F32)

    dft(xh, 0, hs, 0)
    for b in range(last):
        load(1, b).wait() if b < last - 1 else None
        load(2, b).wait() if b < last - 1 else None
        chunks(functools.partial(z_chunk, b), 1 if b == 0 else 0, per)
    for b in range(1, nblk):
        load(0, b).wait() if b < last else None
        load(3, b).wait()
        chunks(functools.partial(g_chunk, b), 0, per)
    learn(0)
    tell(1)
    for b in range(1, nblk):
        dft(xz, b + 1, zs, b + 1)
        dft(xg, b, gs, b)
    learn(1)
    tell(2)

    @pl.when(has_prev)
    def _():
        for copy in to_next:
            copy.wait_recv()

    z_chunk(0, 0)
    g_chunk(0, 0)
    dft(xz, 1, zs, 1)
    dft(xg, 0, gs, 0)
    extra[4].wait()

    def put_spectrum(ref, b, k, lanes, real, imag):
        for off, value in ((0, real), (BLK, imag)):
            high = value.astype(BF16)
            low = (value - high.astype(F32)).astype(BF16)
            ref[b, pl.ds(off + k, ROWS), lanes] = high
            ref[b, pl.ds(2 * BLK + off + k, ROWS), lanes] = low
            ref[b, pl.ds(4 * BLK + off + k, ROWS), lanes] = high

    def by_frequency(body):
        for sign, start in ((1.0, 0), (-1.0, BLK // 2)):
            for lane in range(0, width, 256):

                def step(i, carry, sign=sign, start=start, lane=lane):
                    body(pl.multiple_of(start + i * ROWS, ROWS), slice(lane, lane + 256), sign)
                    return carry

                lax.fori_loop(0, BLK // 2 // ROWS, step, 0)

    def add(a, sign, b):
        return a + b if sign > 0 else a - b

    def z_spectrum(b, start, k, lanes, sign):
        re, im = pl.ds(k, ROWS), pl.ds(BLK + k, ROWS)
        vr = add(zs[b + 1, re, lanes], -sign, zs[b, im, lanes])
        vi = add(zs[b + 1, im, lanes], sign, zs[b, re, lanes])
        hr, hi = hs[0, re, lanes], hs[0, im, lanes]
        put_spectrum(xs, b, k, lanes, hr * vr - hi * vi, hr * vi + hi * vr)
        gr, gi = gs[b, re, lanes], gs[b, im, lanes]
        lr, li = gr * vr + gi * vi, gi * vr - gr * vi
        if not start:
            lr, li = gl_f[re, lanes] + lr, gl_f[im, lanes] + li
        return lr, li

    def z_stage(b, start, final):
        def body(k, lanes, sign):
            lr, li = z_spectrum(b, start, k, lanes, sign)
            if final:
                put_spectrum(xgl, 0, k, lanes, lr, li)
            else:
                gl_f[pl.ds(k, ROWS), lanes] = lr
                gl_f[pl.ds(BLK + k, ROWS), lanes] = li

        by_frequency(body)

    def g_stage(b):
        def body(k, lanes, sign):
            re, im = pl.ds(k, ROWS), pl.ds(BLK + k, ROWS)
            ur = add(gs[b, re, lanes], sign, gs[b + 1, im, lanes])
            ui = add(gs[b, im, lanes], -sign, gs[b + 1, re, lanes])
            hr, hi = hs[0, re, lanes], hs[0, im, lanes]
            put_spectrum(xu, b, k, lanes, hr * ur + hi * ui, hr * ui - hi * ur)

        by_frequency(body)

    def out_rows(b):
        return slice(b * BLK, (b + 1) * BLK)

    for b in range(1, nblk):
        z_stage(b, b == 1, False)
        s_t[out_rows(b), :] = inverse(xs, b)
    for b in range(last):
        g_stage(b)
        gz_t[out_rows(b), :] = inverse(xu, b)

    @pl.when(has_prev)
    def _():
        z_halo.wait_recv()

    xz[0, 2 * BLK :, :] = xz[0, 0:BLK, :]
    dft(xz, 0, zs, 0)
    z_stage(0, False, True)
    gl = inverse(xgl, 0)
    share = BLK // total
    for i in range(total):
        glt[i % 2, i // 2] = gl[share * i : share * (i + 1), :]
    small[9:10, :] = gl[0:1, :]
    to_partner = remote(glt.at[1 - c], gl_in, 8, partner)
    to_partner.start()

    s_t[out_rows(0), :] = inverse(xs, 0)
    row = lax.broadcasted_iota(jnp.int32, (8, width), 0)
    gq8 = yb[0:ROWS, :].astype(F32)[0:8] * s_t[0:8, :]
    gk8 = gz_t[0:8, :] * vf[0:8, :]
    gv8 = gz_t[0:8, :] * kf[0:8, :]
    mine3[...] = jnp.where(row < 2, gq8, jnp.where(row < 4, pltpu.roll(gk8, 2, 0), pltpu.roll(gv8, 4, 0)))
    firsts = remote(mine3, nx, 9, prev)

    @pl.when(has_prev)
    def _():
        firsts.start()

    learn(2)
    to_partner.wait_recv()
    racc[...] = glt[c] + gl_in[...]
    scatter = []
    order = sorted(range(1, chips), key=lambda d: (-min(d, chips - d), d))
    for d in order:
        chip = lax.rem(z + d, chips)
        copy = remote(racc.at[chip], rs_in.at[d], 16 + d, at_chip(chip))
        copy.start()
        scatter.append(copy)

    @pl.when(has_next)
    def _():
        for copy in to_prev + g_halo:
            copy.wait_recv()

    put(xg, nblk, 0, ny[...].astype(F32) * feat(nq[...], qb[tail, :], 0))
    xg[nblk, 2 * BLK + ROWS :, :] = xg[nblk, ROWS:BLK, :]
    dft(xg, nblk, gs, nblk)
    g_stage(last)
    gz_t[out_rows(last), :] = inverse(xu, last)

    def q_rows(row, n):
        return yb[pl.ds(row, ROWS), :].astype(F32)[0:n] * s_t[pl.ds(row, n), :]

    def k_rows(row, n):
        return gz_t[pl.ds(row, n), :] * vf[pl.ds(row, n), :]

    def v_rows(row, n):
        return gz_t[pl.ds(row, n), :] * kf[pl.ds(row, n), :]

    def back(which, rows_of, raw, out, row, after, sums):
        grad = rows_of(row, ROWS)
        cat = jnp.concatenate([grad, rows_of(row + ROWS, 8) if after is None else after], 0)
        one = pltpu.roll(cat, ROWS + 7, 0)[0:ROWS]
        two = pltpu.roll(cat, ROWS + 6, 0)[0:ROWS]
        value = sf[which, 0:1, :] * grad + sf[which, 1:2, :] * one + sf[which, 2:3, :] * two
        out[pl.ds(row, ROWS), :] = value.astype(BF16)
        parts = delayed(raw[pl.ds(row + ROWS, ROWS), :], raw[pl.ds(row, ROWS), :])
        products = [grad * part for part in parts]
        return tuple(s + p[0:8] + p[8:16] for s, p in zip(sums, products))

    kinds = ((0, q_rows, qb, oq), (1, k_rows, kb, ok), (2, v_rows, vb, ov))
    sums = []
    for which, rows_of, raw, out in kinds:

        def step(i, carry, which=which, rows_of=rows_of, raw=raw, out=out):
            return back(which, rows_of, raw, out, pl.multiple_of(i * ROWS, ROWS), None, carry)

        zero = jnp.zeros((8, width), F32)
        sums.append(lax.fori_loop(0, length // ROWS - 1, step, (zero, zero, zero)))

    @pl.when(has_next)
    def _():
        firsts.wait_recv()

    after = nx[...]
    afters = (after, pltpu.roll(after, 6, 0), pltpu.roll(after, 4, 0))
    for (which, rows_of, raw, out), carry, rows in zip(kinds, sums, afters):
        carry = back(which, rows_of, raw, out, length - ROWS, rows, carry)
        for i in range(3):
            small[3 * which + i : 3 * which + i + 1, :] = jnp.sum(carry[i], axis=0, keepdims=True)

    row = lax.broadcasted_iota(jnp.int32, (8, 128), 0)
    for h in range(2):
        lane = 256 * h
        half[h, 0] = small[0:8, lane : lane + 128]
        half[h, 1] = small[0:8, lane + 128 : lane + 256]
        half[h, 2] = jnp.where(
            row < 2,
            small[8:16, lane : lane + 128],
            jnp.where(row < 4, pltpu.roll(small[8:16, lane + 128 : lane + 256], 2, 0), 0.0),
        )
    halves = remote(half.at[1 - c], half_in, 10, partner)
    halves.start()
    halves.wait_recv()
    ar[z] = half[c] + half_in[...]
    spread = []
    for d in order:
        copy = remote(ar.at[z], ar.at[z], 16 + chips + d, at_chip(z + d))
        copy.start()
        spread.append(copy)

    for copy in scatter:
        copy.wait_recv()
    taps = racc[z]
    for d in range(1, chips):
        taps = taps + rs_in[d]
    ofilt[...] = taps

    for copy in spread:
        copy.wait_recv()
    whole = ar[0]
    for chip in range(1, chips):
        whole = whole + ar[chip]
    fin[c] = whole
    final = remote(fin.at[c], fin.at[c], 11, partner)
    final.start()
    final.wait_recv()
    for h in range(2):
        for j in range(2):
            cols = slice(256 * h + 128 * j, 256 * h + 128 * (j + 1))
            for i in range(8):
                otaps[i // 3, i % 3 : i % 3 + 1, cols] = fin[h, j, i : i + 1, :]
            otaps[2, 2:3, cols] = fin[h, 2, 2 * j : 2 * j + 1, :]
            ogain[0:1, cols] = fin[h, 2, 2 * j + 1 : 2 * j + 2, :]

    @pl.when(has_next)
    def _():
        for copy in to_next:
            copy.wait_send()
        z_halo.wait_send()

    @pl.when(has_prev)
    def _():
        for copy in to_prev + g_halo + [firsts]:
            copy.wait_send()

    for copy in [to_partner, halves, final] + scatter + spread:
        copy.wait_send()


def body(fwd, inv, chips, input_q, input_k, input_v, grad_out, short_filters, long_filter, skip_gain):
    length, width = input_q.shape
    nblk = length // BLK
    reach = length + ROWS
    hbm = pl.BlockSpec(memory_space=pl.ANY)
    vmem = pl.BlockSpec(memory_space=pltpu.VMEM)
    scratch = [
        *(pltpu.VMEM((reach, width), BF16) for _ in range(3)),
        pltpu.VMEM((length, width), BF16),
        pltpu.VMEM((ROWS, width), BF16),
        pltpu.VMEM((ROWS, width), BF16),
        pltpu.VMEM(short_filters.shape, F32),
        pltpu.VMEM(long_filter.shape, F32),
        pltpu.VMEM((1, width), F32),
        pltpu.VMEM(fwd.shape, BF16),
        pltpu.VMEM(inv.shape, BF16),
        *(pltpu.VMEM((length, width), F32) for _ in range(4)),
        pltpu.VMEM((nblk + 1, 3 * BLK, width), BF16),
        pltpu.VMEM((nblk + 1, 3 * BLK, width), BF16),
        pltpu.VMEM((1, 3 * BLK, width), BF16),
        pltpu.VMEM((nblk + 1, 2 * BLK, width), F32),
        pltpu.VMEM((nblk + 1, 2 * BLK, width), F32),
        pltpu.VMEM((1, 2 * BLK, width), F32),
        pltpu.VMEM((nblk, 6 * BLK, width), BF16),
        pltpu.VMEM((nblk, 6 * BLK, width), BF16),
        pltpu.VMEM((2 * BLK, width), F32),
        pltpu.VMEM((1, 6 * BLK, width), BF16),
        pltpu.VMEM((8, width), F32),
        pltpu.VMEM((8, width), F32),
        pltpu.VMEM((2, chips, BLK // (2 * chips), width), F32),
        pltpu.VMEM((chips, BLK // (2 * chips), width), F32),
        pltpu.VMEM((chips, BLK // (2 * chips), width), F32),
        pltpu.VMEM((chips, BLK // (2 * chips), width), F32),
        pltpu.VMEM((16, width), F32),
        pltpu.VMEM((2, 3, 8, 128), F32),
        pltpu.VMEM((3, 8, 128), F32),
        pltpu.VMEM((chips, 3, 8, 128), F32),
        pltpu.VMEM((2, 3, 8, 128), F32),
        pltpu.SemaphoreType.DMA((4 * nblk + 5,)),
        pltpu.SemaphoreType.DMA((16 + 2 * chips,)),
        pltpu.SemaphoreType.DMA((16 + 2 * chips,)),
        pltpu.SemaphoreType.REGULAR((3,)),
    ]
    outs = pl.pallas_call(
        functools.partial(kernel, chips),
        out_shape=(
            *(jax.ShapeDtypeStruct((length, width), BF16) for _ in range(3)),
            jax.ShapeDtypeStruct((BLK // (2 * chips), width), F32),
            jax.ShapeDtypeStruct(short_filters.shape, F32),
            jax.ShapeDtypeStruct((1, width), F32),
        ),
        in_specs=[hbm] * 9,
        out_specs=(vmem,) * 6,
        scratch_shapes=scratch,
        compiler_params=pltpu.CompilerParams(
            collective_id=0, has_side_effects=True, vmem_limit_bytes=48 * 1024 * 1024
        ),
        name="hyena_backward",
    )(input_q, input_k, input_v, grad_out, short_filters, long_filter, skip_gain[None], fwd, inv)
    return (*outs[:5], outs[5][0])


def solution(mesh):
    chips = mesh.shape["seq"] // 2
    fwd, inv = tables()

    def run(*arrays):
        return body(jnp.asarray(fwd), jnp.asarray(inv), chips, *arrays)

    return jax.shard_map(
        run,
        mesh=mesh,
        in_specs=(
            P("seq", "ch"),
            P("seq", "ch"),
            P("seq", "ch"),
            P("seq", "ch"),
            P(None, None, "ch"),
            P(None, "ch"),
            P("ch"),
        ),
        out_specs=(
            P("seq", "ch"),
            P("seq", "ch"),
            P("seq", "ch"),
            P("seq", "ch"),
            P(None, None, "ch"),
            P("ch"),
        ),
        check_vma=False,
    )
```

time: 178 us -> 56.6 us (0.32)
  starting transfers between devices: 52.8 us -> 0 us
  matrix products: 45.2 us -> 0 us
  Pallas kernels: 0 us -> 42.9 us
  waiting for transfers between devices: 29.8 us -> 0 us
  local copies, waits for them, and re-layouts: 35.8 us -> 12.5 us
  other arithmetic: 11.6 us -> 0 us
    conv_general_dilated x14 -> x0, matrix products: 45.2 us -> none  [depth_conv(): lax.conv_general_dilated(signal[None], kernel[:, None, :], (1,), 'VALID',...]
    pallas_call x0 -> x1, Pallas kernels: none -> 42.9 us  [body(): pl.pallas_call(functools.partial(kernel, chips), out_shape=(*(jax.ShapeDt...]
    all_to_all x3 -> x0, starting transfers between devices: 39.3 us -> none  [the longest x2 27.1 us: sent_to_all(): lax.all_to_all(jnp.broadcast_to(value[None], (size, *value.shape)), axis,...]
    ppermute x5 -> x0, waiting for transfers between devices: 29.8 us -> none  [shifted(): return lax.ppermute(value, axis, pairs)]
    ppermute x5 -> x0, starting transfers between devices: 13.5 us -> none  [shifted(): return lax.ppermute(value, axis, pairs)]
    conv_general_dilated x29 -> x0, local copies, waits for them, and re-layouts: 12.6 us -> none  [depth_conv(): lax.conv_general_dilated(signal[None], kernel[:, None, :], (1,), 'VALID',...]
    unnamed x56 -> x24, local copies, waits for them, and re-layouts: 5.77 us -> 12.5 us
    convert_element_type x9 -> x0, local copies, waits for them, and re-layouts: 5.33 us -> none  [the longest x3 3 us: body(): back_q = later_filter(grad_q_ext, short_filters[0]).astype(jnp.bfloat16)]
  transfers between devices with their start and end apart: 8 -> 0, of which waited for: 1 -> 0; matrix products, arithmetic and copies ran while one was open for 47% -> 0% of each run, Pallas kernels for 0% -> 0%
where the time goes in v1:
time: 56.6 us; the launch traced here: 56.1 us
  Pallas kernels  42.9 us (76%)
  local copies, waits for them, and re-layouts  12.5 us (22%)
  between operations  0.66 us (1%)
    pallas_call x1, Pallas kernels, body(): pl.pallas_call(functools.partial(kernel, chips), out_shape=(*(jax.ShapeDt...  42.9 us
    unnamed x24, local copies, waits for them, and re-layouts  12.5 us

profile of v1, /device:TPU:1, one launch (start us, length us, event | category | flops | bytes accessed | tf_op | source)
XLA Modules:
  0.0 56.1 jit_solution(11213073621665670056)
XLA Ops:
  0.6 0.0 copy-start
  0.6 1.0 %copy-done = bf16[512,512]{1,0:T(8,128)(2,1)S(1)} copy-done((bf16[512,512]{1,0:T(8,128)(2,1)S(1)}, bf16[512,512]{1,0:T(8,128)(2,1)}, u32[]{:S(2)}) %copy-start) | copy-done | bytes 524312
  1.7 0.0 copy-start.1
  1.7 1.0 %copy-done.1 = bf16[512,512]{1,0:T(8,128)(2,1)S(1)} copy-done((bf16[512,512]{1,0:T(8,128)(2,1)S(1)}, bf16[512,512]{1,0:T(8,128)(2,1)}, u32[]{:S(2)}) %copy-start.1) | copy-done | bytes 524312
  2.7 0.0 copy-start.2
  2.7 1.0 %copy-done.2 = bf16[512,512]{1,0:T(8,128)(2,1)S(1)} copy-done((bf16[512,512]{1,0:T(8,128)(2,1)S(1)}, bf16[512,512]{1,0:T(8,128)(2,1)}, u32[]{:S(2)}) %copy-start.2) | copy-done | bytes 524312
  3.8 0.0 copy-start.3
  3.8 1.0 %copy-done.3 = bf16[512,512]{1,0:T(8,128)(2,1)S(1)} copy-done((bf16[512,512]{1,0:T(8,128)(2,1)S(1)}, bf16[512,512]{1,0:T(8,128)(2,1)}, u32[]{:S(2)}) %copy-start.3) | copy-done | bytes 524312
  4.8 0.0 copy-start.4
  4.8 0.9 %copy-done.4 = f32[128,512]{1,0:T(8,128)S(1)} copy-done((f32[128,512]{1,0:T(8,128)S(1)}, f32[128,512]{1,0:T(8,128)}, u32[]{:S(2)}) %copy-start.4) | copy-done | bytes 262168
  5.8 0.0 copy-start.5
  5.8 0.9 %copy-done.5 = bf16[128,768]{1,0:T(8,128)(2,1)S(1)} copy-done((bf16[128,768]{1,0:T(8,128)(2,1)S(1)}, bf16[128,768]{1,0:T(8,128)(2,1)}, u32[]{:S(2)}) %copy-start.5) | copy-done | bytes 196632
  6.7 0.0 copy-start.6
  6.7 0.9 %copy-done.6 = bf16[256,384]{1,0:T(8,128)(2,1)S(1)} copy-done((bf16[256,384]{1,0:T(8,128)(2,1)S(1)}, bf16[256,384]{1,0:T(8,128)(2,1)}, u32[]{:S(2)}) %copy-start.6) | copy-done | bytes 196632
  7.6 0.0 copy-start.7
  7.6 0.7 %copy-done.7 = f32[3,3,512]{2,1,0:T(4,128)S(1)} copy-done((f32[3,3,512]{2,1,0:T(4,128)S(1)}, f32[3,3,512]{2,1,0:T(4,128)}, u32[]{:S(2)}) %copy-start.7) | copy-done | bytes 18456
  8.3 0.0 copy-start.8
  8.3 0.7 %copy-done.8 = f32[512]{0:T(512)S(1)} copy-done((f32[512]{0:T(512)S(1)}, f32[512]{0:T(512)}, u32[]{:S(2)}) %copy-start.8) | copy-done | bytes 2072
  9.0 42.9 %hyena_backward.1 = (bf16[512,512]{1,0:T(8,128)(2,1)S(1)}, bf16[512,512]{1,0:T(8,128)(2,1)S(1)}, bf16[512,512]{1,0:T(8,128)(2,1)S(1)}, f32[4,512]{1,0:T(4,128)S(...) custom-call(bf16[512,512]{1,0:T(8,128)(2,1)S(1)} %copy-done, bf16[512,512]{1,0:T(8,128)(2,1)S(1)} %copy-done.1, ...), custom_call_target="tpu_custom_call" | custom-call | tf_op jit(solution)/shard_map/hyena_backward/pallas_call | solution.py:504
  51.9 0.8 %copy.21 = bf16[512,512]{1,0:T(8,128)(2,1)} copy(bf16[512,512]{1,0:T(8,128)(2,1)S(1)} %get-tuple-element.24) | data formatting | bytes 1048576
  52.7 0.8 %copy.22 = bf16[512,512]{1,0:T(8,128)(2,1)} copy(bf16[512,512]{1,0:T(8,128)(2,1)S(1)} %get-tuple-element.25) | data formatting | bytes 1048576
  53.5 0.8 %copy.23 = bf16[512,512]{1,0:T(8,128)(2,1)} copy(bf16[512,512]{1,0:T(8,128)(2,1)S(1)} %get-tuple-element.26) | data formatting | bytes 1048576
  54.3 0.6 %copy.24 = f32[4,512]{1,0:T(4,128)} copy(f32[4,512]{1,0:T(4,128)S(1)} %get-tuple-element.27) | data formatting | bytes 16384
  54.9 0.6 %copy.25 = f32[3,3,512]{2,1,0:T(4,128)} copy(f32[3,3,512]{2,1,0:T(4,128)S(1)} %get-tuple-element.28) | data formatting | bytes 36864
  55.5 0.6 %copy.26 = f32[512]{0:T(512)} copy(f32[512]{0:T(512)S(1)} %bitcast.3) | data formatting | bytes 4096
Async XLA Ops:
  0.6 1.0 %copy-start = (bf16[512,512]{1,0:T(8,128)(2,1)S(1)}, bf16[512,512]{1,0:T(8,128)(2,1)}, u32[]{:S(2)}) copy-start(bf16[512,512]{1,0:T(8,128)(2,1)} %q_hbm.1) | copy-start | bytes 1572868
  1.7 1.0 %copy-start.1 = (bf16[512,512]{1,0:T(8,128)(2,1)S(1)}, bf16[512,512]{1,0:T(8,128)(2,1)}, u32[]{:S(2)}) copy-start(bf16[512,512]{1,0:T(8,128)(2,1)} %k_hbm.1) | copy-start | bytes 1572868
  2.7 1.0 %copy-start.2 = (bf16[512,512]{1,0:T(8,128)(2,1)S(1)}, bf16[512,512]{1,0:T(8,128)(2,1)}, u32[]{:S(2)}) copy-start(bf16[512,512]{1,0:T(8,128)(2,1)} %v_hbm.1) | copy-start | bytes 1572868
  3.8 1.0 %copy-start.3 = (bf16[512,512]{1,0:T(8,128)(2,1)S(1)}, bf16[512,512]{1,0:T(8,128)(2,1)}, u32[]{:S(2)}) copy-start(bf16[512,512]{1,0:T(8,128)(2,1)} %y_hbm.1) | copy-start | bytes 1572868
  4.8 0.9 %copy-start.4 = (f32[128,512]{1,0:T(8,128)S(1)}, f32[128,512]{1,0:T(8,128)}, u32[]{:S(2)}) copy-start(f32[128,512]{1,0:T(8,128)} %lf_hbm.1) | copy-start | bytes 786436
  5.8 0.9 %copy-start.5 = (bf16[128,768]{1,0:T(8,128)(2,1)S(1)}, bf16[128,768]{1,0:T(8,128)(2,1)}, u32[]{:S(2)}) copy-start(bf16[128,768]{1,0:T(8,128)(2,1)} %constant.5.clone.inv_hbm) | copy-start | bytes 589828
  6.7 0.9 %copy-start.6 = (bf16[256,384]{1,0:T(8,128)(2,1)S(1)}, bf16[256,384]{1,0:T(8,128)(2,1)}, u32[]{:S(2)}) copy-start(bf16[256,384]{1,0:T(8,128)(2,1)} %constant.4.clone.fwd_hbm) | copy-start | bytes 589828
  7.6 0.7 %copy-start.7 = (f32[3,3,512]{2,1,0:T(4,128)S(1)}, f32[3,3,512]{2,1,0:T(4,128)}, u32[]{:S(2)}) copy-start(f32[3,3,512]{2,1,0:T(4,128)} %sf_hbm.1) | copy-start | bytes 55300
  8.3 0.7 %copy-start.8 = (f32[512]{0:T(512)S(1)}, f32[512]{0:T(512)}, u32[]{:S(2)}) copy-start(f32[512]{0:T(512)} %param.15) | copy-start | bytes 6148

commit v2 on v1

--- a/solution.py
+++ b/solution.py
@@ -458,11 +458,20 @@
         copy.wait_send()
 
 
+def put_out(*refs):
+    sem = refs[-1]
+    copies = [pltpu.make_async_copy(refs[n], refs[n + 6], sem.at[n]) for n in range(6)]
+    for copy in copies:
+        copy.start()
+    for copy in copies:
+        copy.wait()
+
+
 def body(fwd, inv, chips, input_q, input_k, input_v, grad_out, short_filters, long_filter, skip_gain):
     length, width = input_q.shape
     nblk = length // BLK
     reach = length + ROWS
-    hbm = pl.BlockSpec(memory_space=pl.ANY)
+    hbm = pl.BlockSpec(memory_space=pltpu.HBM)
     vmem = pl.BlockSpec(memory_space=pltpu.VMEM)
     scratch = [
         *(pltpu.VMEM((reach, width), BF16) for _ in range(3)),
@@ -501,13 +510,14 @@
         pltpu.SemaphoreType.DMA((16 + 2 * chips,)),
         pltpu.SemaphoreType.REGULAR((3,)),
     ]
+    operands = (input_q, input_k, input_v, grad_out, short_filters, long_filter, skip_gain[None], fwd, inv)
     outs = pl.pallas_call(
         functools.partial(kernel, chips),
         out_shape=(
-            *(jax.ShapeDtypeStruct((length, width), BF16) for _ in range(3)),
-            jax.ShapeDtypeStruct((BLK // (2 * chips), width), F32),
-            jax.ShapeDtypeStruct(short_filters.shape, F32),
-            jax.ShapeDtypeStruct((1, width), F32),
+            *(pltpu.VMEM((length, width), BF16) for _ in range(3)),
+            pltpu.VMEM((BLK // (2 * chips), width), F32),
+            pltpu.VMEM(short_filters.shape, F32),
+            pltpu.VMEM((1, width), F32),
         ),
         in_specs=[hbm] * 9,
         out_specs=(vmem,) * 6,
@@ -516,8 +526,17 @@
             collective_id=0, has_side_effects=True, vmem_limit_bytes=48 * 1024 * 1024
         ),
         name="hyena_backward",
-    )(input_q, input_k, input_v, grad_out, short_filters, long_filter, skip_gain[None], fwd, inv)
-    return (*outs[:5], outs[5][0])
+    )(*(pltpu.with_memory_space_constraint(a, pltpu.HBM) for a in operands))
+    done = pl.pallas_call(
+        put_out,
+        out_shape=tuple(jax.ShapeDtypeStruct(o.shape, o.dtype) for o in outs),
+        in_specs=[vmem] * 6,
+        out_specs=(hbm,) * 6,
+        scratch_shapes=[pltpu.SemaphoreType.DMA((6,))],
+        compiler_params=pltpu.CompilerParams(vmem_limit_bytes=1 << 20),
+        name="put_out",
+    )(*outs)
+    return (*done[:5], done[5][0])
 
 
 def solution(mesh):

time: 56.6 us -> 43 us (0.76)
  local copies, waits for them, and re-layouts: 12.5 us -> 0 us
  Pallas kernels: 42.9 us -> 42.2 us
    unnamed x24 -> x0, local copies, waits for them, and re-layouts: 12.5 us -> none
    pallas_call x1 -> x2, Pallas kernels: 42.9 us -> 42.2 us  [the longest x1 41 us: body(): pl.pallas_call(functools.partial(kernel, chips), out_shape=(*(pltpu.VMEM(...]
where the time goes in v2:
time: 43 us; the launch traced here: 42.9 us
  Pallas kernels  42.2 us (98%)
  between operations  0.64 us (1%)
    pallas_call x1, Pallas kernels, body(): pl.pallas_call(functools.partial(kernel, chips), out_shape=(*(pltpu.VMEM(...  41 us
    pallas_call x1, Pallas kernels, body(): pl.pallas_call(put_out, out_shape=tuple((jax.ShapeDtypeStruct(o.shape, o....  1.2 us

profile of v2, /device:TPU:1, one launch (start us, length us, event | category | flops | bytes accessed | tf_op | source)
XLA Modules:
  0.0 42.9 jit_solution(17362538923498513076)
XLA Ops:
  0.6 41.0 %hyena_backward.1 = (bf16[512,512]{1,0:T(8,128)(2,1)S(1)}, bf16[512,512]{1,0:T(8,128)(2,1)S(1)}, bf16[512,512]{1,0:T(8,128)(2,1)S(1)}, f32[4,512]{1,0:T(4,128)S(...) custom-call(bf16[512,512]{1,0:T(8,128)(2,1)} %q_hbm.1, bf16[512,512]{1,0:T(8,128)(2,1)} %k_hbm.1, ...), custom_call_target="tpu_custom_call" | custom-call | tf_op jit(solution)/shard_map/hyena_backward/pallas_call | solution.py:514
  41.7 1.2 %put_out.1 = (bf16[512,512]{1,0:T(8,128)(2,1)}, bf16[512,512]{1,0:T(8,128)(2,1)}, bf16[512,512]{1,0:T(8,128)(2,1)}, f32[4,512]{1,0:T(4,128)}, f32[3,3,512]{2,1,0:T(4,128)}, /*index=5*/f32[1,512]{1,0:T(1,128)}) custom-call(bf16[512,512]{1,0:T(8,128)(2,1)S(1)} %get-tuple-element.18.refs_0_, bf16[512,512]{1,0:T(8,128)(2,1)S(1)} %get-tuple-element.19.refs_1_, ...), custom_call_target="tpu_custom_call" | custom-call | tf_op jit(solution)/shard_map/put_out/pallas_call | solution.py:530

commit v3 on v2

v3 whole, which is shorter than its diff:
```python
import functools

import jax
import jax.numpy as jnp
import ml_dtypes
import numpy as np
from jax import lax
from jax.experimental import pallas as pl
from jax.experimental.pallas import tpu as pltpu
from jax.sharding import PartitionSpec as P

F32, BF16 = jnp.float32, jnp.bfloat16
BLK = 128
ROWS = 16
PAD = 8
LANES = 128


def tables():
    order = np.concatenate([np.arange(0, BLK, 2), np.arange(1, BLK, 2)])
    angle = np.outer(np.pi * (2 * order + 1) / (2 * BLK), np.arange(BLK))
    full = np.concatenate([np.cos(angle), -np.sin(angle)], 0)
    high = full.astype(ml_dtypes.bfloat16).astype(np.float64)
    low = full - high
    fwd = np.concatenate([high, high, low], 1)
    inv = np.concatenate([high.T, high.T, low.T], 1) / BLK
    return fwd.astype(ml_dtypes.bfloat16), inv.astype(ml_dtypes.bfloat16)


def kernel(
    chips,
    q_hbm, k_hbm, v_hbm, y_hbm, sf_hbm, lf_hbm, sg_hbm, fwd_hbm, inv_hbm,
    oq, ok, ov, ofilt, otaps, ogain,
    qb, kb, vb, yb, hq, hk, hv, nq, ny, sf, lf, sg, fwd, inv,
    rq, rk, rv, rn, kf, vf, gq, gk, gv, xz, xg, xh, zs, gs, hs, xs, xu, gl_f, xgl,
    mine3, nx, glt, gl_in, racc, rs_in, taps, half, half_in, near, far, fin,
    in_sem, send, recv, known,
):
    length = q_hbm.shape[0]
    width = q_hbm.shape[1]
    tiles = width // LANES
    nblk = length // BLK
    last = nblk - 1
    me = lax.axis_index("seq")
    total = 2 * chips
    z, c = me // 2, lax.rem(me, 2)
    has_prev, has_next = me > 0, me < total - 1
    prev, nxt = me - 1, me + 1
    partner = me + 1 - 2 * c

    def at_chip(chip):
        return lax.rem(chip + chips, chips) * 2 + c

    def remote(src, dst, slot, device):
        return pltpu.make_async_remote_copy(
            src_ref=src, dst_ref=dst, send_sem=send.at[slot], recv_sem=recv.at[slot],
            device_id={"seq": device}, device_id_type=pl.DeviceIdType.MESH,
        )

    def signal(sem, device):
        pl.semaphore_signal(sem, 1, device_id={"seq": device}, device_id_type=pl.DeviceIdType.MESH)

    barrier = pltpu.get_barrier_semaphore()
    signal(barrier, at_chip(z + 1))
    signal(barrier, at_chip(z - 1))

    @pl.when(has_prev)
    def _():
        signal(barrier, prev)

    @pl.when(has_next)
    def _():
        signal(barrier, nxt)

    def load(array, b):
        hbm, buf = ((q_hbm, qb), (k_hbm, kb), (v_hbm, vb), (y_hbm, yb))[array]
        rows = pl.ds(b * BLK, BLK)
        return pltpu.make_async_copy(hbm.at[rows], buf.at[rows], in_sem.at[array * nblk + b])

    extra = []
    for n, (hbm, buf) in enumerate(((sf_hbm, sf), (lf_hbm, lf), (sg_hbm, sg), (fwd_hbm, fwd), (inv_hbm, inv))):
        extra.append(pltpu.make_async_copy(hbm, buf, in_sem.at[4 * nblk + n]))

    extra[0].start()
    early = [(1, last - 1), (2, last - 1), (1, last), (2, last), (0, 0), (3, 0), (0, last)]
    for key in early:
        load(*key).start()
    for copy in extra[1:4]:
        copy.start()
    for b in range(nblk):
        for array in (1, 2, 0, 3):
            if (array, b) not in early:
                load(array, b).start()
    extra[4].start()
    waited = set()

    def ready(*keys):
        for key in keys:
            if key not in waited:
                waited.add(key)
                load(*key).wait()

    @pl.when(jnp.logical_not(has_prev))
    def _():
        for buf in (hq, hk, hv):
            buf[...] = jnp.zeros_like(buf)
        xz[0, 0 : 2 * BLK, :] = jnp.zeros((2 * BLK, width), BF16)

    @pl.when(jnp.logical_not(has_next))
    def _():
        nq[...] = jnp.zeros_like(nq)
        ny[...] = jnp.zeros_like(ny)
        xg[nblk, 0 : 2 * BLK, :] = jnp.zeros((2 * BLK, width), BF16)
        nx[...] = jnp.zeros_like(nx)

    for h in range(2):
        half[h, 2] = jnp.zeros((8, LANES), F32)

    def by_tile(body):
        for j in range(tiles):
            body(j, slice(j * LANES, (j + 1) * LANES))

    def weights(which, lanes):
        return [sf[which, i : i + 1, lanes] for i in range(3)]

    def widen(buf, raw, j, lanes, r0, r1):
        raw[j, PAD + r0 : PAD + r1, :] = buf[r0:r1, lanes].astype(F32)

    def feat(raw, j, w, r0, r1):
        return (
            w[0] * raw[j, PAD + r0 : PAD + r1, :]
            + w[1] * raw[j, PAD + r0 - 1 : PAD + r1 - 1, :]
            + w[2] * raw[j, PAD + r0 - 2 : PAD + r1 - 2, :]
        )

    def put(ref, b, n, lanes, value):
        size = value.shape[0]
        high = value.astype(BF16)
        low = (value - high.astype(F32)).astype(BF16)
        ref[b, n : n + size, lanes] = high
        ref[b, BLK + n : BLK + n + size, lanes] = low
        ref[b, 2 * BLK + n : 2 * BLK + n + size, lanes] = high

    def z_rows(b, n0, n1, wide=True):
        def body(j, lanes):
            wk, wv = weights(1, lanes), weights(2, lanes)
            if wide:
                widen(kb, rk, j, lanes, b * BLK + n0, b * BLK + n1)
                widen(vb, rv, j, lanes, b * BLK + n0, b * BLK + n1)
            for n in range(n0, n1, ROWS):
                r0 = b * BLK + n
                kk, vv = feat(rk, j, wk, r0, r0 + ROWS), feat(rv, j, wv, r0, r0 + ROWS)
                kf[j, r0 : r0 + ROWS, :] = kk
                vf[j, r0 : r0 + ROWS, :] = vv
                put(xz, b + 1, n, lanes, kk * vv)

        by_tile(body)

    def g_rows(b, n0, n1, wide=True):
        def body(j, lanes):
            wq = weights(0, lanes)
            if wide:
                widen(qb, rq, j, lanes, b * BLK + n0, b * BLK + n1)
            for n in range(n0, n1, ROWS):
                r0 = b * BLK + n
                put(xg, b, n, lanes, yb[r0 : r0 + ROWS, lanes].astype(F32) * feat(rq, j, wq, r0, r0 + ROWS))

        by_tile(body)

    extra[0].wait()
    ready((1, last - 1), (2, last - 1), (1, last), (2, last))

    def before_last(j, lanes):
        widen(kb, rk, j, lanes, last * BLK - ROWS, last * BLK)
        widen(vb, rv, j, lanes, last * BLK - ROWS, last * BLK)

    by_tile(before_last)
    z_rows(last, 0, BLK)
    ready((0, 0), (3, 0))
    by_tile(lambda j, lanes: widen(qb, rq, j, lanes, 0, ROWS))
    g_rows(0, ROWS, BLK)
    ready((0, last))

    count = 2 + has_prev.astype(jnp.int32) + has_next.astype(jnp.int32)
    pl.semaphore_wait(barrier, count)
    tail = pl.ds(length - PAD, PAD)
    to_next = [remote(buf.at[tail], hist, n, nxt) for n, (buf, hist) in enumerate(((qb, hq), (kb, hk), (vb, hv)))]
    z_halo = remote(xz.at[nblk, pl.ds(0, 2 * BLK)], xz.at[0, pl.ds(0, 2 * BLK)], 3, nxt)
    head = pl.ds(0, ROWS)
    to_prev = [remote(qb.at[head], nq, 4, prev), remote(yb.at[head], ny, 5, prev)]
    g_halo = [
        remote(xg.at[0, pl.ds(h * BLK + ROWS, BLK - ROWS)], xg.at[nblk, pl.ds(h * BLK + ROWS, BLK - ROWS)], 6 + h, prev)
        for h in range(2)
    ]

    @pl.when(has_next)
    def _():
        for copy in to_next:
            copy.start()
        z_halo.start()

    @pl.when(has_prev)
    def _():
        for copy in to_prev + g_halo:
            copy.start()

    steps = []
    radius = 1
    while radius < chips // 2:
        steps.append(radius)
        radius *= 2

    def tell(n):
        if n < len(steps):
            signal(known.at[n], at_chip(z + steps[n]))
            signal(known.at[n], at_chip(z - steps[n]))

    def learn(n):
        if n < len(steps):
            pl.semaphore_wait(known.at[n], 2)

    tell(0)

    for b in range(nblk):
        ready((0, b), (1, b), (2, b), (3, b))
    for copy in extra[1:]:
        copy.wait()
    for b in range(last):
        if b == 0:
            by_tile(lambda j, lanes: (widen(kb, rk, j, lanes, 0, ROWS), widen(vb, rv, j, lanes, 0, ROWS)))
        z_rows(b, ROWS if b == 0 else 0, BLK)
    for b in range(1, nblk):
        g_rows(b, 0, BLK)


    def filter_rows(j, lanes):
        first = lf[0:ROWS, lanes]
        at_zero = lax.broadcasted_iota(jnp.int32, (ROWS, LANES), 0) == 0
        put(xh, 0, 0, lanes, jnp.where(at_zero, first + sg[:, lanes], first))
        put(xh, 0, ROWS, lanes, lf[ROWS:BLK, lanes])

    by_tile(filter_rows)

    def dft(x, b, out, o):
        for lane in range(0, width, 256):
            cols = slice(lane, lane + 256)
            out[o, :, cols] = jnp.dot(fwd[...], x[b, :, cols], preferred_element_type=F32)

    dft(xh, 0, hs, 0)
    for b in range(1, nblk):
        dft(xz, b + 1, zs, b + 1)
        dft(xg, b, gs, b)
    learn(0)
    tell(1)
    @pl.when(has_prev)
    def _():
        for copy in to_next:
            copy.wait_recv()

    def history(j, lanes):
        for raw, hist in ((rq, hq), (rk, hk), (rv, hv)):
            raw[j, 0:PAD, :] = hist[:, lanes].astype(F32)

    by_tile(history)
    z_rows(0, 0, ROWS, False)
    g_rows(0, 0, ROWS, False)
    dft(xz, 1, zs, 1)
    dft(xg, 0, gs, 0)

    def put_spectrum(ref, b, k, lanes, real, imag):
        for off, value in ((0, real), (BLK, imag)):
            high = value.astype(BF16)
            low = (value - high.astype(F32)).astype(BF16)
            ref[b, off + k : off + k + ROWS, lanes] = high
            ref[b, 2 * BLK + off + k : 2 * BLK + off + k + ROWS, lanes] = low
            ref[b, 4 * BLK + off + k : 4 * BLK + off + k + ROWS, lanes] = high

    def add(a, sign, b):
        return a + b if sign > 0 else a - b

    def frequencies():
        for k in range(0, BLK, ROWS):
            yield k, slice(k, k + ROWS), slice(BLK + k, BLK + k + ROWS), 1 if k < BLK // 2 else -1

    def z_stage(blocks, final):
        def body(j, lanes):
            for k, re, im, sign in frequencies():
                hr, hi = hs[0, re, lanes], hs[0, im, lanes]
                lr = li = None
                if final:
                    lr, li = gl_f[re, lanes], gl_f[im, lanes]
                for b in blocks:
                    vr = add(zs[b + 1, re, lanes], -sign, zs[b, im, lanes])
                    vi = add(zs[b + 1, im, lanes], sign, zs[b, re, lanes])
                    gr, gi = gs[b, re, lanes], gs[b, im, lanes]
                    pr, pi = gr * vr + gi * vi, gi * vr - gr * vi
                    lr, li = (pr, pi) if lr is None else (lr + pr, li + pi)
                    put_spectrum(xs, b, k, lanes, hr * vr - hi * vi, hr * vi + hi * vr)
                if final:
                    put_spectrum(xgl, 0, k, lanes, lr, li)
                else:
                    gl_f[re, lanes] = lr
                    gl_f[im, lanes] = li

        by_tile(body)

    def g_stage(blocks):
        def body(j, lanes):
            for k, re, im, sign in frequencies():
                hr, hi = hs[0, re, lanes], hs[0, im, lanes]
                for b in blocks:
                    ur = add(gs[b, re, lanes], sign, gs[b + 1, im, lanes])
                    ui = add(gs[b, im, lanes], -sign, gs[b + 1, re, lanes])
                    put_spectrum(xu, b, k, lanes, hr * ur + hi * ui, hr * ui - hi * ur)

        by_tile(body)

    def inverse(x, b, use):
        for lane in range(0, width, 256):
            value = jnp.dot(inv[...], x[b, :, lane : lane + 256], preferred_element_type=F32)
            for part in range(0, 256, LANES):
                use(b, (lane + part) // LANES, value[:, part : part + LANES])

    def use_s(b, j, value):
        rows = slice(b * BLK, (b + 1) * BLK)
        gq[j, rows, :] = value * yb[rows, LANES * j : LANES * (j + 1)].astype(F32)

    def use_gz(b, j, value):
        rows = slice(b * BLK, (b + 1) * BLK)
        gk[j, rows, :] = value * vf[j, rows, :]
        gv[j, rows, :] = value * kf[j, rows, :]

    kinds = ((gq, rq, oq), (gk, rk, ok), (gv, rv, ov))

    def finish(which, r0, r1, fresh=False, write=True, count=True):
        grad, raw, out = kinds[which]

        def body(j, lanes):
            w = weights(which, lanes)
            sums = [None if fresh else taps[3 * which + i, j] for i in range(3)] if count else None
            for r in range(r0, r1, ROWS):
                own = grad[j, r : r + ROWS, :]
                if write:
                    one, two = grad[j, r + 1 : r + 1 + ROWS, :], grad[j, r + 2 : r + 2 + ROWS, :]
                    out[r : r + ROWS, lanes] = (w[0] * own + w[1] * one + w[2] * two).astype(BF16)
                if count:
                    for i in range(3):
                        product = own * raw[j, PAD + r - i : PAD + r - i + ROWS, :]
                        product = product[0:8] + product[8:16]
                        sums[i] = product if sums[i] is None else sums[i] + product
            if count:
                for i in range(3):
                    taps[3 * which + i, j] = sums[i]

        by_tile(body)

    z_stage(range(1, nblk), False)
    g_stage(range(last))
    for b in range(1, nblk):
        inverse(xs, b, use_s)
    for b in range(last):
        inverse(xu, b, use_gz)
    finish(0, BLK, length - ROWS, True)
    finish(0, length - ROWS, length, write=False)
    for which in (1, 2):
        finish(which, 0, last * BLK - ROWS, True)

    learn(1)
    tell(2)

    @pl.when(has_prev)
    def _():
        z_halo.wait_recv()

    @pl.when(has_next)
    def _():
        for copy in to_prev + g_halo:
            copy.wait_recv()

    share = BLK // total

    def next_rows(j, lanes):
        w = weights(0, lanes)
        rn[j, 0:PAD, :] = rq[j, length : length + PAD, :]
        rn[j, PAD : PAD + ROWS, :] = nq[:, lanes].astype(F32)
        put(xg, nblk, 0, lanes, ny[:, lanes].astype(F32) * feat(rn, j, w, 0, ROWS))

    def use_gl(b, j, value):
        cols = slice(LANES * j, LANES * (j + 1))
        for i in range(total):
            glt[i % 2, i // 2, :, cols] = value[share * i : share * (i + 1), :]
        half[j // 2, 2, 2 * (j % 2) + 1 : 2 * (j % 2) + 2, :] = value[0:1, :]

    xz[0, 2 * BLK :, :] = xz[0, 0:BLK, :]
    by_tile(next_rows)
    xg[nblk, 2 * BLK + ROWS :, :] = xg[nblk, ROWS:BLK, :]
    dft(xz, 0, zs, 0)
    dft(xg, nblk, gs, nblk)
    z_stage((0,), True)
    g_stage((last,))
    inverse(xs, 0, use_s)
    inverse(xgl, 0, use_gl)
    inverse(xu, last, use_gz)
    row = lax.broadcasted_iota(jnp.int32, (8, LANES), 0)
    for j in range(tiles):
        second, third = pltpu.roll(gk[j, 0:8, :], 2, 0), pltpu.roll(gv[j, 0:8, :], 4, 0)
        mine3[j] = jnp.where(row < 2, gq[j, 0:8, :], jnp.where(row < 4, second, third))
    to_partner = remote(glt.at[1 - c], gl_in, 8, partner)
    to_partner.start()
    finish(0, 0, BLK)
    for which in (1, 2):
        finish(which, last * BLK - ROWS, length - ROWS)
        finish(which, length - ROWS, length, write=False)
    for j in range(tiles):
        h, jj = j // 2, j % 2
        for n in range(9):
            total_n = jnp.sum(taps[n, j], axis=0, keepdims=True)
            if n < 8:
                half[h, jj, n : n + 1, :] = total_n
            else:
                half[h, 2, 2 * jj : 2 * jj + 1, :] = total_n
    halves = remote(half.at[1 - c], half_in, 10, partner)
    halves.start()
    firsts = remote(mine3, nx, 9, prev)

    @pl.when(has_prev)
    def _():
        firsts.start()

    to_partner.wait_recv()
    racc[...] = glt[c] + gl_in[...]
    halves.wait_recv()
    group = min(4, chips)
    base = z // group * group
    place = z - base
    near[place] = half[c] + half_in[...]
    close = []
    for d in range(1, group):
        copy = remote(near.at[place], near.at[place], 16 + chips + d, at_chip(base + lax.rem(place + d, group)))
        copy.start()
        close.append(copy)
    learn(2)
    order = sorted(range(1, chips), key=lambda d: (-min(d, chips - d), d))
    cut = 5 if chips == 16 else 1
    scatter = []

    def send_taps(distances):
        for d in distances:
            chip = lax.rem(z + d, chips)
            copy = remote(racc.at[chip], rs_in.at[d], 16 + d, at_chip(chip))
            copy.start()
            scatter.append(copy)

    send_taps(order[:cut])
    @pl.when(has_next)
    def _():
        firsts.wait_recv()

    for j in range(tiles):
        gq[j, length : length + 8, :] = nx[j]
        gk[j, length : length + 8, :] = pltpu.roll(nx[j], 6, 0)
        gv[j, length : length + 8, :] = pltpu.roll(nx[j], 4, 0)
    for which in range(3):
        finish(which, length - ROWS, length, count=False)

    for copy in close:
        copy.wait_recv()
    mine = z // group
    summed = near[0]
    for n in range(1, group):
        summed = summed + near[n]
    far[mine] = summed
    groups = chips // group
    distant = []
    for d in range(1, groups):
        copy = remote(far.at[mine], far.at[mine], 20 + chips + d, at_chip(z + d * group))
        copy.start()
        distant.append(copy)
    send_taps(order[cut:])

    for copy in scatter:
        copy.wait_recv()
    mine_taps = racc[z]
    for d in range(1, chips):
        mine_taps = mine_taps + rs_in[d]
    ofilt[...] = mine_taps

    for copy in distant:
        copy.wait_recv()
    whole = far[0]
    for n in range(1, groups):
        whole = whole + far[n]
    fin[c] = whole
    final = remote(fin.at[c], fin.at[c], 11, partner)
    final.start()
    final.wait_recv()
    for h in range(2):
        for j in range(2):
            cols = slice(256 * h + 128 * j, 256 * h + 128 * (j + 1))
            for i in range(8):
                otaps[i // 3, i % 3 : i % 3 + 1, cols] = fin[h, j, i : i + 1, :]
            otaps[2, 2:3, cols] = fin[h, 2, 2 * j : 2 * j + 1, :]
            ogain[0:1, cols] = fin[h, 2, 2 * j + 1 : 2 * j + 2, :]

    @pl.when(has_next)
    def _():
        for copy in to_next:
            copy.wait_send()
        z_halo.wait_send()

    @pl.when(has_prev)
    def _():
        for copy in to_prev + g_halo + [firsts]:
            copy.wait_send()

    for copy in [to_partner, halves, final] + close + distant + scatter:
        copy.wait_send()


def put_out(*refs):
    sem = refs[-1]
    copies = [pltpu.make_async_copy(refs[n], refs[n + 6], sem.at[n]) for n in range(6)]
    for copy in copies:
        copy.start()
    for copy in copies:
        copy.wait()


def body(fwd, inv, chips, input_q, input_k, input_v, grad_out, short_filters, long_filter, skip_gain):
    length, width = input_q.shape
    nblk = length // BLK
    hbm = pl.BlockSpec(memory_space=pltpu.HBM)
    vmem = pl.BlockSpec(memory_space=pltpu.VMEM)
    tiles = width // LANES
    share = BLK // (2 * chips)
    scratch = [
        *(pltpu.VMEM((length, width), BF16) for _ in range(4)),
        *(pltpu.VMEM((PAD, width), BF16) for _ in range(3)),
        *(pltpu.VMEM((ROWS, width), BF16) for _ in range(2)),
        pltpu.VMEM(short_filters.shape, F32),
        pltpu.VMEM(long_filter.shape, F32),
        pltpu.VMEM((1, width), F32),
        pltpu.VMEM(fwd.shape, BF16),
        pltpu.VMEM(inv.shape, BF16),
        *(pltpu.VMEM((tiles, PAD + length, LANES), F32) for _ in range(3)),
        pltpu.VMEM((tiles, PAD + ROWS, LANES), F32),
        *(pltpu.VMEM((tiles, length, LANES), F32) for _ in range(2)),
        *(pltpu.VMEM((tiles, length + 8, LANES), F32) for _ in range(3)),
        pltpu.VMEM((nblk + 1, 3 * BLK, width), BF16),
        pltpu.VMEM((nblk + 1, 3 * BLK, width), BF16),
        pltpu.VMEM((1, 3 * BLK, width), BF16),
        pltpu.VMEM((nblk + 1, 2 * BLK, width), F32),
        pltpu.VMEM((nblk + 1, 2 * BLK, width), F32),
        pltpu.VMEM((1, 2 * BLK, width), F32),
        pltpu.VMEM((nblk, 6 * BLK, width), BF16),
        pltpu.VMEM((nblk, 6 * BLK, width), BF16),
        pltpu.VMEM((2 * BLK, width), F32),
        pltpu.VMEM((1, 6 * BLK, width), BF16),
        pltpu.VMEM((tiles, 8, LANES), F32),
        pltpu.VMEM((tiles, 8, LANES), F32),
        pltpu.VMEM((2, chips, share, width), F32),
        pltpu.VMEM((chips, share, width), F32),
        pltpu.VMEM((chips, share, width), F32),
        pltpu.VMEM((chips, share, width), F32),
        pltpu.VMEM((9, tiles, 8, LANES), F32),
        pltpu.VMEM((2, 3, 8, LANES), F32),
        pltpu.VMEM((3, 8, LANES), F32),
        pltpu.VMEM((4, 3, 8, LANES), F32),
        pltpu.VMEM((4, 3, 8, LANES), F32),
        pltpu.VMEM((2, 3, 8, LANES), F32),
        pltpu.SemaphoreType.DMA((4 * nblk + 5,)),
        pltpu.SemaphoreType.DMA((32 + chips,)),
        pltpu.SemaphoreType.DMA((32 + chips,)),
        pltpu.SemaphoreType.REGULAR((3,)),
    ]
    operands = (input_q, input_k, input_v, grad_out, short_filters, long_filter, skip_gain[None], fwd, inv)
    outs = pl.pallas_call(
        functools.partial(kernel, chips),
        out_shape=(
            *(pltpu.VMEM((length, width), BF16) for _ in range(3)),
            pltpu.VMEM((BLK // (2 * chips), width), F32),
            pltpu.VMEM(short_filters.shape, F32),
            pltpu.VMEM((1, width), F32),
        ),
        in_specs=[hbm] * 9,
        out_specs=(vmem,) * 6,
        scratch_shapes=scratch,
        compiler_params=pltpu.CompilerParams(
            collective_id=0, has_side_effects=True, vmem_limit_bytes=48 * 1024 * 1024
        ),
        name="hyena_backward",
    )(*(pltpu.with_memory_space_constraint(a, pltpu.HBM) for a in operands))
    done = pl.pallas_call(
        put_out,
        out_shape=tuple(jax.ShapeDtypeStruct(o.shape, o.dtype) for o in outs),
        in_specs=[vmem] * 6,
        out_specs=(hbm,) * 6,
        scratch_shapes=[pltpu.SemaphoreType.DMA((6,))],
        compiler_params=pltpu.CompilerParams(vmem_limit_bytes=1 << 20),
        name="put_out",
    )(*outs)
    return (*done[:5], done[5][0])


def solution(mesh):
    chips = mesh.shape["seq"] // 2
    fwd, inv = tables()

    def run(*arrays):
        return body(jnp.asarray(fwd), jnp.asarray(inv), chips, *arrays)

    return jax.shard_map(
        run,
        mesh=mesh,
        in_specs=(
            P("seq", "ch"),
            P("seq", "ch"),
            P("seq", "ch"),
            P("seq", "ch"),
            P(None, None, "ch"),
            P(None, "ch"),
            P("ch"),
        ),
        out_specs=(
            P("seq", "ch"),
            P("seq", "ch"),
            P("seq", "ch"),
            P("seq", "ch"),
            P(None, None, "ch"),
            P("ch"),
        ),
        check_vma=False,
    )
```

time: 43 us -> 37.5 us (0.87)
  Pallas kernels: 42.2 us -> 36.7 us
    pallas_call x1, Pallas kernels: 41 us -> 35.5 us  [body(): pl.pallas_call(functools.partial(kernel, chips), out_shape=(*(pltpu.VMEM(...]
where the time goes in v3:
time: 37.5 us; the launch traced here: 37.3 us
  Pallas kernels  36.7 us (98%)
  between operations  0.64 us (2%)
    pallas_call x1, Pallas kernels, body(): pl.pallas_call(functools.partial(kernel, chips), out_shape=(*(pltpu.VMEM(...  35.5 us
    pallas_call x1, Pallas kernels, body(): pl.pallas_call(put_out, out_shape=tuple((jax.ShapeDtypeStruct(o.shape, o....  1.2 us

profile of v3, /device:TPU:1, one launch (start us, length us, event | category | flops | bytes accessed | tf_op | source)
XLA Modules:
  0.0 37.3 jit_solution(16005533194019245926)
XLA Ops:
  0.6 35.5 %hyena_backward.1 = (bf16[512,512]{1,0:T(8,128)(2,1)S(1)}, bf16[512,512]{1,0:T(8,128)(2,1)S(1)}, bf16[512,512]{1,0:T(8,128)(2,1)S(1)}, f32[4,512]{1,0:T(4,128)S(...) custom-call(bf16[512,512]{1,0:T(8,128)(2,1)} %q_hbm.1, bf16[512,512]{1,0:T(8,128)(2,1)} %k_hbm.1, ...), custom_call_target="tpu_custom_call" | custom-call | tf_op jit(solution)/shard_map/hyena_backward/pallas_call | solution.py:577
  36.1 1.2 %put_out.1 = (bf16[512,512]{1,0:T(8,128)(2,1)}, bf16[512,512]{1,0:T(8,128)(2,1)}, bf16[512,512]{1,0:T(8,128)(2,1)}, f32[4,512]{1,0:T(4,128)}, f32[3,3,512]{2,1,0:T(4,128)}, /*index=5*/f32[1,512]{1,0:T(1,128)}) custom-call(bf16[512,512]{1,0:T(8,128)(2,1)S(1)} %get-tuple-element.18.refs_0_, bf16[512,512]{1,0:T(8,128)(2,1)S(1)} %get-tuple-element.19.refs_1_, ...), custom_call_target="tpu_custom_call" | custom-call | tf_op jit(solution)/shard_map/put_out/pallas_call | solution.py:593

commit v4 on v3

--- a/solution.py
+++ b/solution.py
@@ -225,33 +225,34 @@
         ready((0, b), (1, b), (2, b), (3, b))
     for copy in extra[1:]:
         copy.wait()
-    for b in range(last):
-        if b == 0:
-            by_tile(lambda j, lanes: (widen(kb, rk, j, lanes, 0, ROWS), widen(vb, rv, j, lanes, 0, ROWS)))
-        z_rows(b, ROWS if b == 0 else 0, BLK)
-    for b in range(1, nblk):
-        g_rows(b, 0, BLK)
-
-
     def filter_rows(j, lanes):
         first = lf[0:ROWS, lanes]
         at_zero = lax.broadcasted_iota(jnp.int32, (ROWS, LANES), 0) == 0
         put(xh, 0, 0, lanes, jnp.where(at_zero, first + sg[:, lanes], first))
         put(xh, 0, ROWS, lanes, lf[ROWS:BLK, lanes])
 
-    by_tile(filter_rows)
-
     def dft(x, b, out, o):
         for lane in range(0, width, 256):
             cols = slice(lane, lane + 256)
             out[o, :, cols] = jnp.dot(fwd[...], x[b, :, cols], preferred_element_type=F32)
 
+    by_tile(lambda j, lanes: (widen(kb, rk, j, lanes, 0, ROWS), widen(vb, rv, j, lanes, 0, ROWS)))
+    by_tile(filter_rows)
+    g_rows(1, 0, BLK)
     dft(xh, 0, hs, 0)
-    for b in range(1, nblk):
-        dft(xz, b + 1, zs, b + 1)
-        dft(xg, b, gs, b)
+    dft(xz, nblk, zs, nblk)
+    z_rows(0, ROWS, BLK)
+    dft(xg, 1, gs, 1)
+    z_rows(1, 0, BLK)
+    g_rows(2, 0, BLK)
+    dft(xz, 2, zs, 2)
     learn(0)
     tell(1)
+    z_rows(2, 0, BLK)
+    dft(xg, 2, gs, 2)
+    g_rows(last, 0, BLK)
+    dft(xz, last, zs, last)
+    dft(xg, last, gs, last)
     @pl.when(has_prev)
     def _():
         for copy in to_next:
@@ -282,12 +283,12 @@
         for k in range(0, BLK, ROWS):
             yield k, slice(k, k + ROWS), slice(BLK + k, BLK + k + ROWS), 1 if k < BLK // 2 else -1
 
-    def z_stage(blocks, final):
+    def z_stage(blocks, mode):
         def body(j, lanes):
             for k, re, im, sign in frequencies():
                 hr, hi = hs[0, re, lanes], hs[0, im, lanes]
                 lr = li = None
-                if final:
+                if mode != "first":
                     lr, li = gl_f[re, lanes], gl_f[im, lanes]
                 for b in blocks:
                     vr = add(zs[b + 1, re, lanes], -sign, zs[b, im, lanes])
@@ -296,7 +297,7 @@
                     pr, pi = gr * vr + gi * vi, gi * vr - gr * vi
                     lr, li = (pr, pi) if lr is None else (lr + pr, li + pi)
                     put_spectrum(xs, b, k, lanes, hr * vr - hi * vi, hr * vi + hi * vr)
-                if final:
+                if mode == "last":
                     put_spectrum(xgl, 0, k, lanes, lr, li)
                 else:
                     gl_f[re, lanes] = lr
@@ -354,19 +355,30 @@
 
         by_tile(body)
 
-    z_stage(range(1, nblk), False)
-    g_stage(range(last))
-    for b in range(1, nblk):
-        inverse(xs, b, use_s)
-    for b in range(last):
-        inverse(xu, b, use_gz)
-    finish(0, BLK, length - ROWS, True)
-    finish(0, length - ROWS, length, write=False)
-    for which in (1, 2):
-        finish(which, 0, last * BLK - ROWS, True)
-
+    z_stage((1,), "first")
     learn(1)
     tell(2)
+    z_stage((2,), "more")
+    inverse(xs, 1, use_s)
+    z_stage((3,), "more")
+    inverse(xs, 2, use_s)
+    g_stage((0,))
+    inverse(xs, 3, use_s)
+    finish(0, BLK, 3 * BLK - ROWS, True)
+    g_stage((1,))
+    inverse(xu, 0, use_gz)
+    finish(0, 3 * BLK - ROWS, length - ROWS)
+    finish(0, length - ROWS, length, write=False)
+    g_stage((2,))
+    inverse(xu, 1, use_gz)
+    finish(1, 0, BLK - ROWS, True)
+    finish(2, 0, BLK - ROWS, True)
+    inverse(xu, 2, use_gz)
+    finish(1, BLK - ROWS, 2 * BLK - ROWS)
+    finish(2, BLK - ROWS, 2 * BLK - ROWS)
+    finish(1, 2 * BLK - ROWS, 3 * BLK - ROWS)
+    finish(2, 2 * BLK - ROWS, 3 * BLK - ROWS)
+
 
     @pl.when(has_prev)
     def _():
@@ -396,7 +408,7 @@
     xg[nblk, 2 * BLK + ROWS :, :] = xg[nblk, ROWS:BLK, :]
     dft(xz, 0, zs, 0)
     dft(xg, nblk, gs, nblk)
-    z_stage((0,), True)
+    z_stage((0,), "last")
     g_stage((last,))
     inverse(xs, 0, use_s)
     inverse(xgl, 0, use_gl)
@@ -432,26 +444,22 @@
     halves.wait_recv()
     group = min(4, chips)
     base = z // group * group
-    place = z - base
-    near[place] = half[c] + half_in[...]
-    close = []
-    for d in range(1, group):
-        copy = remote(near.at[place], near.at[place], 16 + chips + d, at_chip(base + lax.rem(place + d, group)))
+    place, mine = z - base, z // group
+    groups = chips // group
+    learn(2)
+    far[mine] = half[c] + half_in[...]
+    distant = []
+    for d in sorted(range(1, groups), key=lambda d: -min(d, groups - d)):
+        copy = remote(far.at[mine], far.at[mine], 20 + chips + d, at_chip(z + d * group))
         copy.start()
-        close.append(copy)
-    learn(2)
-    order = sorted(range(1, chips), key=lambda d: (-min(d, chips - d), d))
-    cut = 5 if chips == 16 else 1
+        distant.append(copy)
     scatter = []
-
-    def send_taps(distances):
-        for d in distances:
-            chip = lax.rem(z + d, chips)
-            copy = remote(racc.at[chip], rs_in.at[d], 16 + d, at_chip(chip))
-            copy.start()
-            scatter.append(copy)
-
-    send_taps(order[:cut])
+    for d in sorted(range(1, chips), key=lambda d: (-min(d, chips - d), d)):
+        chip = lax.rem(z + d, chips)
+        copy = remote(racc.at[chip], rs_in.at[d], 16 + d, at_chip(chip))
+        copy.start()
+        scatter.append(copy)
+
     @pl.when(has_next)
     def _():
         firsts.wait_recv()
@@ -463,20 +471,17 @@
     for which in range(3):
         finish(which, length - ROWS, length, count=False)
 
-    for copy in close:
+    for copy in distant:
         copy.wait_recv()
-    mine = z // group
-    summed = near[0]
-    for n in range(1, group):
-        summed = summed + near[n]
-    far[mine] = summed
-    groups = chips // group
-    distant = []
-    for d in range(1, groups):
-        copy = remote(far.at[mine], far.at[mine], 20 + chips + d, at_chip(z + d * group))
+    summed = far[0]
+    for n in range(1, groups):
+        summed = summed + far[n]
+    near[place] = summed
+    close = []
+    for d in range(1, group):
+        copy = remote(near.at[place], near.at[place], 16 + chips + d, at_chip(base + lax.rem(place + d, group)))
         copy.start()
-        distant.append(copy)
-    send_taps(order[cut:])
+        close.append(copy)
 
     for copy in scatter:
         copy.wait_recv()
@@ -485,11 +490,11 @@
         mine_taps = mine_taps + rs_in[d]
     ofilt[...] = mine_taps
 
-    for copy in distant:
+    for copy in close:
         copy.wait_recv()
-    whole = far[0]
-    for n in range(1, groups):
-        whole = whole + far[n]
+    whole = near[0]
+    for n in range(1, group):
+        whole = whole + near[n]
     fin[c] = whole
     final = remote(fin.at[c], fin.at[c], 11, partner)
     final.start()

time: 37.5 us -> 35.7 us (0.952)
  Pallas kernels: 36.7 us -> 34.9 us
    pallas_call x1, Pallas kernels: 35.5 us -> 33.7 us  [body(): pl.pallas_call(functools.partial(kernel, chips), out_shape=(*(pltpu.VMEM(...]
where the time goes in v4:
time: 35.7 us; the launch traced here: 35.5 us
  Pallas kernels  34.9 us (98%)
  between operations  0.64 us (2%)
    pallas_call x1, Pallas kernels, body(): pl.pallas_call(functools.partial(kernel, chips), out_shape=(*(pltpu.VMEM(...  33.7 us
    pallas_call x1, Pallas kernels, body(): pl.pallas_call(put_out, out_shape=tuple((jax.ShapeDtypeStruct(o.shape, o....  1.2 us

profile of v4, /device:TPU:1, one launch (start us, length us, event | category | flops | bytes accessed | tf_op | source)
XLA Modules:
  0.0 35.5 jit_solution(12582940907727960918)
XLA Ops:
  0.6 33.7 %hyena_backward.1 = (bf16[512,512]{1,0:T(8,128)(2,1)S(1)}, bf16[512,512]{1,0:T(8,128)(2,1)S(1)}, bf16[512,512]{1,0:T(8,128)(2,1)S(1)}, f32[4,512]{1,0:T(4,128)S(...) custom-call(bf16[512,512]{1,0:T(8,128)(2,1)} %q_hbm.1, bf16[512,512]{1,0:T(8,128)(2,1)} %k_hbm.1, ...), custom_call_target="tpu_custom_call" | custom-call | tf_op jit(solution)/shard_map/hyena_backward/pallas_call | solution.py:582
  34.3 1.2 %put_out.1 = (bf16[512,512]{1,0:T(8,128)(2,1)}, bf16[512,512]{1,0:T(8,128)(2,1)}, bf16[512,512]{1,0:T(8,128)(2,1)}, f32[4,512]{1,0:T(4,128)}, f32[3,3,512]{2,1,0:T(4,128)}, /*index=5*/f32[1,512]{1,0:T(1,128)}) custom-call(bf16[512,512]{1,0:T(8,128)(2,1)S(1)} %get-tuple-element.18.refs_0_, bf16[512,512]{1,0:T(8,128)(2,1)S(1)} %get-tuple-element.19.refs_1_, ...), custom_call_target="tpu_custom_call" | custom-call | tf_op jit(solution)/shard_map/put_out/pallas_call | solution.py:598

commit v5 on v4

--- a/solution.py
+++ b/solution.py
@@ -356,40 +356,68 @@
         by_tile(body)
 
     z_stage((1,), "first")
+    z_stage((2,), "more")
+    z_stage((3,), "more")
     learn(1)
     tell(2)
-    z_stage((2,), "more")
+
+    @pl.when(has_prev)
+    def _():
+        z_halo.wait_recv()
+
+    share = BLK // total
+
+    def use_gl(b, j, value):
+        cols = slice(LANES * j, LANES * (j + 1))
+        for i in range(total):
+            glt[i % 2, i // 2, :, cols] = value[share * i : share * (i + 1), :]
+        half[j // 2, 2, 2 * (j % 2) + 1 : 2 * (j % 2) + 2, :] = value[0:1, :]
+
+    xz[0, 2 * BLK :, :] = xz[0, 0:BLK, :]
+    dft(xz, 0, zs, 0)
+    z_stage((0,), "last")
+    inverse(xgl, 0, use_gl)
+    to_partner = remote(glt.at[1 - c], gl_in, 8, partner)
+    to_partner.start()
+    inverse(xs, 0, use_s)
+    g_stage((0,))
+    inverse(xu, 0, use_gz)
+    g_stage((1,))
+    row = lax.broadcasted_iota(jnp.int32, (8, LANES), 0)
+    for j in range(tiles):
+        second, third = pltpu.roll(gk[j, 0:8, :], 2, 0), pltpu.roll(gv[j, 0:8, :], 4, 0)
+        mine3[j] = jnp.where(row < 2, gq[j, 0:8, :], jnp.where(row < 4, second, third))
+    firsts = remote(mine3, nx, 9, prev)
+
+    @pl.when(has_prev)
+    def _():
+        firsts.start()
+
     inverse(xs, 1, use_s)
-    z_stage((3,), "more")
-    inverse(xs, 2, use_s)
-    g_stage((0,))
-    inverse(xs, 3, use_s)
-    finish(0, BLK, 3 * BLK - ROWS, True)
-    g_stage((1,))
-    inverse(xu, 0, use_gz)
-    finish(0, 3 * BLK - ROWS, length - ROWS)
-    finish(0, length - ROWS, length, write=False)
-    g_stage((2,))
     inverse(xu, 1, use_gz)
+    finish(0, 0, BLK - ROWS, True)
     finish(1, 0, BLK - ROWS, True)
     finish(2, 0, BLK - ROWS, True)
-    inverse(xu, 2, use_gz)
-    finish(1, BLK - ROWS, 2 * BLK - ROWS)
-    finish(2, BLK - ROWS, 2 * BLK - ROWS)
-    finish(1, 2 * BLK - ROWS, 3 * BLK - ROWS)
-    finish(2, 2 * BLK - ROWS, 3 * BLK - ROWS)
-
-
-    @pl.when(has_prev)
-    def _():
-        z_halo.wait_recv()
+    to_partner.wait_recv()
+    racc[...] = glt[c] + gl_in[...]
+    learn(2)
+    order = sorted(range(1, chips), key=lambda d: (-min(d, chips - d), d))
+    cut = 4 if chips == 16 else 1
+    scatter = []
+
+    def send_taps(distances):
+        for d in distances:
+            chip = lax.rem(z + d, chips)
+            copy = remote(racc.at[chip], rs_in.at[d], 16 + d, at_chip(chip))
+            copy.start()
+            scatter.append(copy)
+
+    send_taps(order[:cut])
 
     @pl.when(has_next)
     def _():
         for copy in to_prev + g_halo:
             copy.wait_recv()
-
-    share = BLK // total
 
     def next_rows(j, lanes):
         w = weights(0, lanes)
@@ -397,31 +425,22 @@
         rn[j, PAD : PAD + ROWS, :] = nq[:, lanes].astype(F32)
         put(xg, nblk, 0, lanes, ny[:, lanes].astype(F32) * feat(rn, j, w, 0, ROWS))
 
-    def use_gl(b, j, value):
-        cols = slice(LANES * j, LANES * (j + 1))
-        for i in range(total):
-            glt[i % 2, i // 2, :, cols] = value[share * i : share * (i + 1), :]
-        half[j // 2, 2, 2 * (j % 2) + 1 : 2 * (j % 2) + 2, :] = value[0:1, :]
-
-    xz[0, 2 * BLK :, :] = xz[0, 0:BLK, :]
     by_tile(next_rows)
     xg[nblk, 2 * BLK + ROWS :, :] = xg[nblk, ROWS:BLK, :]
-    dft(xz, 0, zs, 0)
+    g_stage((2,))
     dft(xg, nblk, gs, nblk)
-    z_stage((0,), "last")
+    inverse(xs, 2, use_s)
+    inverse(xu, 2, use_gz)
+    finish(0, BLK - ROWS, 2 * BLK - ROWS)
+    inverse(xs, 3, use_s)
     g_stage((last,))
-    inverse(xs, 0, use_s)
-    inverse(xgl, 0, use_gl)
+    finish(1, BLK - ROWS, 2 * BLK - ROWS)
+    finish(2, BLK - ROWS, 2 * BLK - ROWS)
     inverse(xu, last, use_gz)
-    row = lax.broadcasted_iota(jnp.int32, (8, LANES), 0)
-    for j in range(tiles):
-        second, third = pltpu.roll(gk[j, 0:8, :], 2, 0), pltpu.roll(gv[j, 0:8, :], 4, 0)
-        mine3[j] = jnp.where(row < 2, gq[j, 0:8, :], jnp.where(row < 4, second, third))
-    to_partner = remote(glt.at[1 - c], gl_in, 8, partner)
-    to_partner.start()
-    finish(0, 0, BLK)
+    finish(0, 2 * BLK - ROWS, length - ROWS)
+    finish(0, length - ROWS, length, write=False)
     for which in (1, 2):
-        finish(which, last * BLK - ROWS, length - ROWS)
+        finish(which, 2 * BLK - ROWS, length - ROWS)
         finish(which, length - ROWS, length, write=False)
     for j in range(tiles):
         h, jj = j // 2, j % 2
@@ -433,32 +452,18 @@
                 half[h, 2, 2 * jj : 2 * jj + 1, :] = total_n
     halves = remote(half.at[1 - c], half_in, 10, partner)
     halves.start()
-    firsts = remote(mine3, nx, 9, prev)
-
-    @pl.when(has_prev)
-    def _():
-        firsts.start()
-
-    to_partner.wait_recv()
-    racc[...] = glt[c] + gl_in[...]
     halves.wait_recv()
     group = min(4, chips)
     base = z // group * group
     place, mine = z - base, z // group
     groups = chips // group
-    learn(2)
     far[mine] = half[c] + half_in[...]
     distant = []
     for d in sorted(range(1, groups), key=lambda d: -min(d, groups - d)):
         copy = remote(far.at[mine], far.at[mine], 20 + chips + d, at_chip(z + d * group))
         copy.start()
         distant.append(copy)
-    scatter = []
-    for d in sorted(range(1, chips), key=lambda d: (-min(d, chips - d), d)):
-        chip = lax.rem(z + d, chips)
-        copy = remote(racc.at[chip], rs_in.at[d], 16 + d, at_chip(chip))
-        copy.start()
-        scatter.append(copy)
+    send_taps(order[cut:])
 
     @pl.when(has_next)
     def _():

time: 35.7 us -> 37.2 us (1.042)
  Pallas kernels: 34.9 us -> 36.4 us
    pallas_call x1, Pallas kernels: 33.7 us -> 35.2 us  [body(): pl.pallas_call(functools.partial(kernel, chips), out_shape=(*(pltpu.VMEM(...]
where the time goes in v5:
time: 37.2 us; the launch traced here: 37.1 us
  Pallas kernels  36.4 us (98%)
  between operations  0.64 us (2%)
    pallas_call x1, Pallas kernels, body(): pl.pallas_call(functools.partial(kernel, chips), out_shape=(*(pltpu.VMEM(...  35.2 us
    pallas_call x1, Pallas kernels, body(): pl.pallas_call(put_out, out_shape=tuple((jax.ShapeDtypeStruct(o.shape, o....  1.2 us

profile of v5, /device:TPU:1, one launch (start us, length us, event | category | flops | bytes accessed | tf_op | source)
XLA Modules:
  0.0 37.1 jit_solution(5408169932736660589)
XLA Ops:
  0.6 35.2 %hyena_backward.1 = (bf16[512,512]{1,0:T(8,128)(2,1)S(1)}, bf16[512,512]{1,0:T(8,128)(2,1)S(1)}, bf16[512,512]{1,0:T(8,128)(2,1)S(1)}, f32[4,512]{1,0:T(4,128)S(...) custom-call(bf16[512,512]{1,0:T(8,128)(2,1)} %q_hbm.1, bf16[512,512]{1,0:T(8,128)(2,1)} %k_hbm.1, ...), custom_call_target="tpu_custom_call" | custom-call | tf_op jit(solution)/shard_map/hyena_backward/pallas_call | solution.py:587
  35.9 1.2 %put_out.1 = (bf16[512,512]{1,0:T(8,128)(2,1)}, bf16[512,512]{1,0:T(8,128)(2,1)}, bf16[512,512]{1,0:T(8,128)(2,1)}, f32[4,512]{1,0:T(4,128)}, f32[3,3,512]{2,1,0:T(4,128)}, /*index=5*/f32[1,512]{1,0:T(1,128)}) custom-call(bf16[512,512]{1,0:T(8,128)(2,1)S(1)} %get-tuple-element.18.refs_0_, bf16[512,512]{1,0:T(8,128)(2,1)S(1)} %get-tuple-element.19.refs_1_, ...), custom_call_target="tpu_custom_call" | custom-call | tf_op jit(solution)/shard_map/put_out/pallas_call | solution.py:603

commit v6 on v4

--- a/solution.py
+++ b/solution.py
@@ -356,13 +356,13 @@
         by_tile(body)
 
     z_stage((1,), "first")
-    learn(1)
-    tell(2)
     z_stage((2,), "more")
     inverse(xs, 1, use_s)
     z_stage((3,), "more")
     inverse(xs, 2, use_s)
     g_stage((0,))
+    learn(1)
+    tell(2)
     inverse(xs, 3, use_s)
     finish(0, BLK, 3 * BLK - ROWS, True)
     g_stage((1,))

time: 35.7 us -> 35.4 us (level)
  no operation moved by 1% of the time
where the time goes in v6:
time: 35.4 us; the launch traced here: 35.3 us
  Pallas kernels  34.6 us (98%)
  between operations  0.64 us (2%)
    pallas_call x1, Pallas kernels, body(): pl.pallas_call(functools.partial(kernel, chips), out_shape=(*(pltpu.VMEM(...  33.4 us
    pallas_call x1, Pallas kernels, body(): pl.pallas_call(put_out, out_shape=tuple((jax.ShapeDtypeStruct(o.shape, o....  1.2 us

profile of v6, /device:TPU:1, one launch (start us, length us, event | category | flops | bytes accessed | tf_op | source)
XLA Modules:
  0.0 35.3 jit_solution(8738331692632897197)
XLA Ops:
  0.6 33.4 %hyena_backward.1 = (bf16[512,512]{1,0:T(8,128)(2,1)S(1)}, bf16[512,512]{1,0:T(8,128)(2,1)S(1)}, bf16[512,512]{1,0:T(8,128)(2,1)S(1)}, f32[4,512]{1,0:T(4,128)S(...) custom-call(bf16[512,512]{1,0:T(8,128)(2,1)} %q_hbm.1, bf16[512,512]{1,0:T(8,128)(2,1)} %k_hbm.1, ...), custom_call_target="tpu_custom_call" | custom-call | tf_op jit(solution)/shard_map/hyena_backward/pallas_call | solution.py:582
  34.1 1.2 %put_out.1 = (bf16[512,512]{1,0:T(8,128)(2,1)}, bf16[512,512]{1,0:T(8,128)(2,1)}, bf16[512,512]{1,0:T(8,128)(2,1)}, f32[4,512]{1,0:T(4,128)}, f32[3,3,512]{2,1,0:T(4,128)}, /*index=5*/f32[1,512]{1,0:T(1,128)}) custom-call(bf16[512,512]{1,0:T(8,128)(2,1)S(1)} %get-tuple-element.18.refs_0_, bf16[512,512]{1,0:T(8,128)(2,1)S(1)} %get-tuple-element.19.refs_1_, ...), custom_call_target="tpu_custom_call" | custom-call | tf_op jit(solution)/shard_map/put_out/pallas_call | solution.py:598
